TPU v7x, 256 devices: a whole 4x4x8 slice. The times are simulated.
256 devices in a mesh: blk: 32 (over x, z), help: 8 (over y, core).
Axes of the slice: x: 4, y: 4, z: 8, core: 2. Of those that a mesh axis runs over, the one named last changes fastest.
Arguments:
- source_points: float32 [32, 1024, 128], P('blk'), may hold values from -4.5 to 4.5
- source_potential: float32 [32, 1024], P('blk'), may hold values from -3 to 3
- target_points: float32 [32, 1024, 128], P('blk', 'help'), may hold values from -4.5 to 4.5
- target_potential: float32 [32, 1024], P('blk', 'help'), may hold values from -3 to 3
- pairs: int32 [32, 16], P('blk'), may hold values from 0 to 31, as said below
- counts: int32 [32], P('blk'), may hold values from 1 to 16, as said below
- owner: int32 [32], replicated, may hold values from 0 to 31, each once
Outputs:
- new_source_points: float32 [32, 1024, 128], P('blk')
- new_source_potential: float32 [32, 1024], P('blk')
- new_target_points: float32 [32, 1024, 128], P('blk', 'help')
- new_target_potential: float32 [32, 1024], P('blk', 'help')
Inputs may be any that keep to these rules, and one draw needn't show every extreme that they name: `pairs`: each row names 16 different clusters; every cluster is named in a live slot of some row. `counts`: every draw has a block with all 16 slots live.
All inputs are finite; a program needn't handle non-finite values.
Results may differ from a plain program's by a relative error of at most 0.019.
Values may be sent and summed in bfloat16 or wider, within the bound.
No kernel may reach another device: no remote copies, remote signals or barrier semaphores. Data moves between devices by JAX's collectives and lax.ppermute only.
A program may use at most 64 MiB of HBM per device.

v0:
```python
import functools

import jax
import jax.numpy as jnp
from jax import lax
from jax.experimental import pallas as pl
from jax.experimental.pallas import tpu as pltpu
from jax.sharding import Mesh
from jax.sharding import PartitionSpec as P

ITERS = 2
HELP = ("y", "c")
SHARD = 128
WIDTH = 128
SIDE = SHARD + 16
MSG = 2 * SIDE
META = 8
SQUARE = 9
LIMIT = 40.0
XS, ZS, YS, CS = 4, 8, 4, 2
TEMPER = 0.25
STRIDE = 0.5
LOW = -1e30

F32 = jnp.float32
BF16 = jnp.bfloat16
LANES = (((1,), (1,)), ((), ()))


def as_row(column):
    return jnp.broadcast_to(column, (SHARD, WIDTH)).T[:16]


def in_three(rows):
    hi = rows.astype(BF16)
    rest = rows - hi.astype(F32)
    mid = rest.astype(BF16)
    lo = (rest - mid.astype(F32)).astype(BF16)
    at = lax.broadcasted_iota(jnp.int32, rows.shape, 0)
    out = jnp.where(at == 0, hi.astype(F32), jnp.where(at == 1, mid.astype(F32), lo.astype(F32)))
    return jnp.where(at < 3, out, 0.0)


def of_three(rows):
    rows = rows.astype(F32)
    return rows[0:1] + rows[1:2] + rows[2:3]


def square_row(rounded):
    wide = rounded.astype(F32)
    return as_row(jnp.sum(wide * wide, axis=1, keepdims=True))


def write_side(msg_ref, copies_ref, source_ref, side, points, level_row, meta=None):
    rounded = points.astype(BF16)
    square = square_row(rounded)
    bias = level_row * (1.0 / TEMPER) - square * (1.0 / (WIDTH * TEMPER))
    at = lax.broadcasted_iota(jnp.int32, square.shape, 0)
    extras = jnp.where(at == SQUARE, square, in_three(bias))
    if meta is not None:
        extras = jnp.where(at == META, meta, extras)
    extras = extras.astype(BF16)
    msg_ref[pl.ds(side * SIDE, SHARD), :] = rounded
    msg_ref[pl.ds(side * SIDE + SHARD, 16), :] = extras
    if side == 0:
        for k in range(copies_ref.shape[0]):
            copies_ref[k, pl.ds(0, SHARD), :] = rounded
            copies_ref[k, pl.ds(SHARD, 16), :] = extras
    else:
        source_ref[pl.ds(0, SHARD), :] = rounded
        source_ref[pl.ds(SHARD, 16), :] = extras


def prepare_kernel(
    at_ref, pairs_ref, counts_ref, owner_ref, tp_ref, tl_ref, sp_ref, sl_ref, msg_ref, copies_ref, source_ref
):
    lane = lax.broadcasted_iota(jnp.int32, (1, WIDTH), 1)
    meta = jnp.zeros((1, WIDTH), F32)
    count = counts_ref[0]
    for slot in range(pairs_ref.shape[1]):
        partner = jnp.where(slot < count, owner_ref[pairs_ref[0, slot]], -1)
        meta = jnp.where(lane == partner, 1.0, meta)
    write_side(msg_ref, copies_ref, source_ref, 0, tp_ref[0], tl_ref[...], meta)
    write_side(msg_ref, copies_ref, source_ref, 1, sp_ref[0], sl_ref[...])


def attend_kernel(at_ref, pairs_ref, counts_ref, owner_ref, named_ref, *refs):
    far, ring, helpers = XS, ZS, YS * CS
    target_refs, refs = refs[:far], refs[far:]
    source_refs, refs = refs[:ring], refs[ring:]
    query_refs, refs = [ref.at[n] for ref in refs[:2] for n in range(helpers // 2)], refs[2:]
    *out_refs, list_ref, key_ref, scaled_ref, shift_ref, sum_ref, acc_ref = refs
    at_x, at_z = at_ref[0], at_ref[1]
    blocks = far * ring
    for k in range(ring):
        key_ref[pl.ds(k * far, far)] = source_refs[k][...]
    for k in range(far):
        key_ref[pl.ds(blocks + k * ring, ring)] = target_refs[k][...]

    def largest(extras):
        top = functools.reduce(jnp.maximum, extras).astype(F32)
        return jnp.max(top[SQUARE : SQUARE + 1])

    bound = largest([key_ref[j, pl.ds(SHARD, 16), :] for j in range(2 * blocks)]) * largest(
        [ref[pl.ds(at, 16), :] for ref in query_refs for at in (SHARD, SIDE + SHARD)]
    )
    safe = bound * 1.03 <= (LIMIT * WIDTH * TEMPER / 2.0) ** 2

    def enlist_sources(j, count):
        list_ref[0, count] = ((at_z - j) & (ring - 1)) * far + j // ring
        return count + jnp.where(named_ref[j] > 0, 1, 0)

    def enlist_targets(s, carry):
        block = owner_ref[pairs_ref[0, s]]
        list_ref[1, s] = blocks + ((at_x - block // ring) & (far - 1)) * ring + (block & (ring - 1))
        return carry

    naming = lax.fori_loop(0, blocks, enlist_sources, 0)
    lax.fori_loop(0, pairs_ref.shape[1], enlist_targets, 0)

    def one_side(side, carry):
        q_at = pl.multiple_of(side * SIDE, 16)
        live = jnp.where(side == 0, naming, counts_ref[0])
        list_ref[side, live] = list_ref[side, 0]
        for c in range(helpers):
            scaled_ref[pl.ds(c * SHARD, SHARD), :] = query_refs[c][pl.ds(q_at, SHARD), :] * jnp.asarray(
                2.0 / (WIDTH * TEMPER), BF16
            )
        sum_ref[...] = jnp.zeros(sum_ref.shape, F32)
        acc_ref[...] = jnp.zeros(acc_ref.shape, F32)
        turns = (live + 1) // 2

        def biases(t):
            left = of_three(key_ref[list_ref[side, 2 * t], pl.ds(SHARD, 16), :])
            right = of_three(key_ref[list_ref[side, 2 * t + 1], pl.ds(SHARD, 16), :])
            return left, jnp.where(2 * t + 1 < live, right, LOW)

        def scores(t, shift, rows):
            first = key_ref[list_ref[side, 2 * t], pl.ds(0, SHARD), :]
            second = key_ref[list_ref[side, 2 * t + 1], pl.ds(0, SHARD), :]
            key = jnp.concatenate([first, second], axis=0)
            left, right = biases(t)
            cross = lax.dot_general(scaled_ref[rows, :], key, LANES, preferred_element_type=F32)
            return cross[:, :SHARD] + (left - shift), cross[:, SHARD:] + (right - shift), key

        def add(left, right, key, rows):
            left = jnp.exp(left)
            right = jnp.exp(right)
            sum_ref[rows, :] += left + right
            weight = jnp.concatenate([left.astype(BF16), right.astype(BF16)], axis=1)
            acc_ref[rows, :] += jnp.dot(weight, key, preferred_element_type=F32)

        @pl.when(safe)
        def _():
            def top_bias(t, top):
                left, right = biases(t)
                return jnp.maximum(top, jnp.maximum(left, right))

            top = lax.fori_loop(0, turns, top_bias, jnp.full((1, WIDTH), LOW, F32))
            top = jnp.max(top, axis=1, keepdims=True)
            shift_ref[...] = jnp.broadcast_to(top, shift_ref.shape)

            def add_up(t, carry):
                rows = pl.ds(0, helpers * SHARD)
                add(*scores(t, top, rows), rows)
                return carry

            lax.fori_loop(0, turns, add_up, 0)

        @pl.when(jnp.logical_not(safe))
        def _():
            def one_part(c, carry):
                rows = pl.ds(pl.multiple_of(c * SHARD, SHARD), SHARD)

                def find_peak(t, peak):
                    left, right, _ = scores(t, 0.0, rows)
                    return jnp.maximum(peak, jnp.maximum(left, right))

                peak = lax.fori_loop(0, turns, find_peak, jnp.full((SHARD, WIDTH), LOW, F32))
                top = jnp.broadcast_to(jnp.max(peak, axis=1, keepdims=True), (SHARD, WIDTH))
                shift_ref[:, rows] = top.T[:16]

                def add_up(t, carry):
                    left, right, key = scores(t, 0.0, rows)
                    add(left - top, right - top, key, rows)
                    return carry

                return lax.fori_loop(0, turns, add_up, carry)

            lax.fori_loop(0, helpers, one_part, 0)

        whole = sum_ref[...]
        hi = whole.astype(BF16)
        mid = (whole - hi.astype(F32)).astype(BF16)
        ones = jnp.ones((WIDTH, WIDTH), BF16)
        across = jnp.dot(hi, ones, preferred_element_type=F32) + jnp.dot(mid, ones, preferred_element_type=F32)
        mean = (acc_ref[...] * (1.0 / across)).astype(BF16)
        few = jnp.ones((16, WIDTH), BF16)
        total = lax.dot_general(few, hi, LANES, preferred_element_type=F32)
        total += lax.dot_general(few, mid, LANES, preferred_element_type=F32)
        lse = in_three(shift_ref[...] + jnp.log(total)).astype(BF16)
        for c in range(helpers):
            rows = slice(c * SHARD, (c + 1) * SHARD)
            out_ref, to = out_refs[c % CS], c // CS
            out_ref[to, pl.ds(q_at, SHARD), :] = mean[rows]
            out_ref[to, pl.ds(pl.multiple_of(q_at + SHARD, 16), 16), :] = lse[:, rows]
        return carry

    lax.fori_loop(0, 2, one_side, 0)


def merge_kernel(own_ref, other_ref, *refs):
    *out_refs, scr_ref = refs
    cases = [(k, side * SIDE) for k in range(len(out_refs)) for side in range(2)]
    scr_ref[...] = jnp.zeros(scr_ref.shape, F32)
    for n, (k, at) in enumerate(cases):
        own = of_three(own_ref[k, pl.ds(at + SHARD, 16), :])
        other = of_three(other_ref[k, pl.ds(at + SHARD, 16), :])
        top = jnp.maximum(own, other)
        share = jnp.exp(own - top)
        total = share + jnp.exp(other - top)
        scr_ref[pl.ds(n, 1), :] = share / total
        lse = jnp.broadcast_to(top + jnp.log(total), (16, SHARD))
        out_refs[k][pl.ds(at + SHARD, 16), :] = in_three(lse).astype(BF16)
    columns = scr_ref[...].T
    for n, (k, at) in enumerate(cases):
        own = own_ref[k, pl.ds(at, SHARD), :].astype(F32)
        other = other_ref[k, pl.ds(at, SHARD), :].astype(F32)
        out_refs[k][pl.ds(at, SHARD), :] = (other + columns[:, n : n + 1] * (own - other)).astype(BF16)


def settle_kernel(*refs):
    got_refs, refs = refs[:YS], refs[YS:]
    tp_ref, sp_ref, ntp_ref, level_ref, nsp_ref, *msg_refs, scr_ref = refs
    for side, old_ref, new_ref in ((0, tp_ref, ntp_ref), (1, sp_ref, nsp_ref)):
        at = side * SIDE
        parts = [of_three(ref[pl.ds(at + SHARD, 16), :]) for ref in got_refs]
        top = functools.reduce(jnp.maximum, parts)
        shares = [jnp.exp(part - top) for part in parts]
        total = functools.reduce(jnp.add, shares)
        scr_ref[...] = jnp.zeros(scr_ref.shape, F32)
        for h, share in enumerate(shares):
            scr_ref[pl.ds(h, 1), :] = share / total
        columns = scr_ref[...].T
        mean = jnp.zeros((SHARD, WIDTH), F32)
        for h, ref in enumerate(got_refs):
            mean = mean + columns[:, h : h + 1] * ref[pl.ds(at, SHARD), :].astype(F32)
        old = old_ref[pl.ds(0, SHARD), :]
        square = square_row(old.astype(BF16))
        level = -TEMPER * (top + jnp.log(total) - square * (1.0 / (WIDTH * TEMPER)))
        new = old + STRIDE * (mean - old)
        new_ref[pl.ds(0, SHARD), :] = new
        if side:
            new_ref[pl.ds(SHARD, 8), :] = level[:8]
        else:
            level_ref[...] = level[:1]
        if msg_refs:
            write_side(*msg_refs, side, new, level)


def finish_kernel(at_ref, *refs):
    own_ref, other_ref, points_ref, level_ref = refs
    for n in range(YS * CS):
        ref = (own_ref, other_ref)[n % CS].at[n // CS]
        helper = ((at_ref[2] - n // CS) & (YS - 1)) * CS + ((at_ref[3] + n) & (CS - 1))
        points_ref[0, pl.ds(pl.multiple_of(helper * SHARD, SHARD), SHARD), :] = ref[pl.ds(0, SHARD), :]
        level_ref[pl.ds(helper, 1), :] = ref[pl.ds(SHARD, 1), :]


def near_core(*arrays):
    return [pltpu.with_memory_space_constraint(x, pltpu.VMEM) for x in arrays]


def exchanged(copies, axes):
    return lax.all_to_all(copies, axes, split_axis=0, concat_axis=0, tiled=True)


def shifted(x, axis, step):
    n = lax.axis_size(axis)
    return lax.ppermute(x, axis, [(i, (i + step) % n) for i in range(n)])


def crossed(x, axis, bit):
    return lax.ppermute(x, axis, [(i, i ^ bit) for i in range(lax.axis_size(axis))])


def from_helpers(msg):
    near = jnp.stack([msg, crossed(msg, "c", 1)])
    near = jnp.concatenate([near, crossed(near, "y", 1)])
    return near, crossed(near, "y", 2)


def from_helpers_late(msg):
    own = jnp.stack([shifted(msg, "y", k) if k else msg for k in range(YS)])
    return own, shifted(own, "c", 1)


def from_blocks(copies, source):
    sides = [source] + [shifted(source, "x", k) for k in range(1, XS)]
    near = exchanged(copies, "z")
    ring = [None] * ZS
    ring[0] = ahead = back = jnp.stack(sides)
    targets = [near]
    for k in range(1, XS):
        targets.append(shifted(near, "x", k))
    for k in range(1, ZS // 2 + 1):
        ring[k] = ahead = shifted(ahead, "z", 1)
        if k < ZS // 2:
            ring[ZS - k] = back = shifted(back, "z", ZS - 1)
    return targets, ring


def on_device(
    source_points, source_potential, target_points, target_potential, pairs, counts, owner
):
    helper = lax.axis_index(HELP)
    block = lax.axis_index(("x", "z"))
    blocks = XS * ZS
    helpers = YS * CS
    at = jnp.stack([lax.axis_index(axis) for axis in ("x", "z", "y", "c")])
    smem = pl.BlockSpec(memory_space=pltpu.SMEM)
    vmem = pl.BlockSpec(memory_space=pltpu.VMEM)
    msg_shape = pltpu.VMEM((MSG, WIDTH), BF16)
    copies_shape = pltpu.VMEM((ZS, SIDE, WIDTH), BF16)
    source_shape = pltpu.VMEM((SIDE, WIDTH), BF16)
    half_shape = pltpu.VMEM((YS, MSG, WIDTH), BF16)
    final_shape = pltpu.VMEM((SHARD + 8, WIDTH), F32)
    own_points = pl.BlockSpec((1, SHARD, WIDTH), lambda i, at: (0, at[2] * CS + at[3], 0))
    own_level = pl.BlockSpec((1, SHARD), lambda i, at: (0, at[2] * CS + at[3]))
    whole = lambda *shape: pl.BlockSpec(shape, lambda i, at: (0,) * len(shape))
    msg, copies, source = pl.pallas_call(
        prepare_kernel,
        out_shape=(msg_shape, copies_shape, source_shape),
        grid_spec=pltpu.PrefetchScalarGridSpec(
            num_scalar_prefetch=1,
            grid=(1,),
            in_specs=[smem, smem, smem, whole(1, SHARD, WIDTH), whole(1, SHARD), own_points, own_level],
            out_specs=(whole(*msg_shape.shape), whole(*copies_shape.shape), whole(*source_shape.shape)),
        ),
        name="prepare",
    )(at, pairs, counts, owner, target_points, target_potential, source_points, source_potential)
    tp = target_points[0]
    sp = lax.dynamic_slice_in_dim(source_points[0], helper * SHARD, SHARD, 0)
    points_shape = jax.ShapeDtypeStruct((SHARD, WIDTH), F32)
    kept_shape = pltpu.VMEM((SHARD, WIDTH), F32)
    level_shape = jax.ShapeDtypeStruct((1, SHARD), F32)
    named = None
    for step in range(ITERS):
        targets, sources = from_blocks(copies, source)
        query = from_helpers(msg)
        if named is None:
            meta = jnp.concatenate([part[:, SHARD + META, :blocks] for part in targets])
            named = lax.dynamic_index_in_dim(meta, block, 1, False).astype(jnp.int32)
        own, other = pl.pallas_call(
            attend_kernel,
            out_shape=(half_shape, half_shape),
            in_specs=[smem] * 5 + [vmem] * (XS + ZS + 2),
            out_specs=(vmem, vmem),
            scratch_shapes=[
                pltpu.SMEM((2, blocks + 1), jnp.int32),
                pltpu.VMEM((2 * blocks, SIDE, WIDTH), BF16),
                pltpu.VMEM((helpers * SHARD, WIDTH), BF16),
                pltpu.VMEM((16, helpers * SHARD), F32),
                pltpu.VMEM((helpers * SHARD, WIDTH), F32),
                pltpu.VMEM((helpers * SHARD, WIDTH), F32),
            ],
            name="attend",
        )(
            at, pairs, counts, owner, named,
            targets[0], *near_core(*targets[1:]),
            *sources[: ZS // 2], *near_core(*sources[ZS // 2 : ZS // 2 + 2]), *sources[ZS // 2 + 2 :],
            query[0], *near_core(*query[1:]),
        )
        other = shifted(other, "c", 1)
        merged = pl.pallas_call(
            merge_kernel,
            out_shape=(msg_shape,) * YS,
            in_specs=[vmem, vmem],
            out_specs=(vmem,) * YS,
            scratch_shapes=[pltpu.VMEM((WIDTH, SHARD), F32)],
            name="merge",
        )(*near_core(own, other))
        got = [crossed(part, "y", k) if k else part for k, part in enumerate(merged)]
        last = step == ITERS - 1
        messages = () if last else (msg_shape, copies_shape, source_shape)
        tp, tl, sp, *rest = pl.pallas_call(
            settle_kernel,
            out_shape=(points_shape if last else kept_shape, level_shape, final_shape, *messages),
            in_specs=[vmem] * (YS + 2),
            out_specs=(vmem,) * (3 + len(messages)),
            scratch_shapes=[pltpu.VMEM((WIDTH, SHARD), F32)],
            name="settle",
        )(*near_core(*got), *((tp, sp) if step == 0 else near_core(tp, sp)))
        msg, copies, source = rest or (None,) * 3
    new_source_points, new_source_potential = pl.pallas_call(
        finish_kernel,
        out_shape=(jax.ShapeDtypeStruct(source_points.shape, F32), jax.ShapeDtypeStruct((helpers, SHARD), F32)),
        in_specs=[smem, vmem, vmem],
        out_specs=(vmem, vmem),
        name="finish",
    )(at, *near_core(*from_helpers_late(sp)))
    return new_source_points, new_source_potential.reshape(source_potential.shape), tp[None], tl


def solution(mesh):
    torus = Mesh(mesh.devices.reshape(XS, ZS, YS, CS), ("x", "z", "y", "c"))
    blk = ("x", "z")
    in_specs = (
        P(blk, None, None),
        P(blk, None),
        P(blk, HELP, None),
        P(blk, HELP),
        P(blk, None),
        P(blk),
        P(),
    )
    out_specs = (P(blk, None, None), P(blk, None), P(blk, HELP, None), P(blk, HELP))
    return jax.shard_map(
        on_device, mesh=torus, in_specs=in_specs, out_specs=out_specs, check_vma=False
    )
```

profile of v0, /device:TPU:1, one launch (start us, length us, event | category | flops | bytes accessed | tf_op | source)
XLA Modules:
  0.0 194.5 jit_solution(10999040881631484372)
XLA Ops:
  1.9 2.4 %prepare.1 = (bf16[288,128]{1,0:T(8,128)(2,1)S(1)}, bf16[8,144,128]{2,1,0:T(8,128)(2,1)}, bf16[144,128]{1,0:T(8,128)(2,1)S(1)}) custom-call(s32[4]{0:T(128)} %pad_add_fusion.at_ref, s32[1,16]{1,0:T(1,128)} %pairs_ref.5, s32[1]{0:T(128)S(6)} %copy.32.counts_ref, s32[32]{0:T(128)} %owner_ref.5, f32[1,128,128]{2,1,0:T(8,128)} %tp_ref.1, f32[1,128]{1,0:T(1,128)} %tl_ref.1, ...), custom_call_target="tpu_custom_call" | custom-call | tf_op jit(solution)/shard_map/prepare/pallas_call | solution.py:331
  4.3 3.3 %collective-permute-start.5 = (bf16[144,128]{1,0:T(8,128)(2,1)S(1)}, bf16[144,128]{1,0:T(8,128)(2,1)S(1)}, u32[]{:S(2)}, u32[]{:S(2)}) collective-permute-start(bf16[144,128]{1,0:T(8,128)(2,1)S(1)} %get-tuple-element.30), channel_id=1, source_target_pairs={{0,192},{64,0},{128,64},{192,128},{1,193},{65,1},{129,65},{193,129... | collective-permute-start | bytes 110600 | tf_op jit(solution)/shard_map/ppermute | solution.py:280
  8.8 8.2 %all-to-all-start = ((bf16[8,144,128]{2,1,0:T(8,128)(2,1)}), bf16[8,144,128]{2,1,0:T(8,128)(2,1)S(1)}, u32[]{:S(2)}, u32[]{:S(2)}) async-start(bf16[8,144,128]{2,1,0:T(8,128)(2,1)} %get-tuple-element.29), calls=%async_computation | async-start | bytes 589824 | tf_op jit(solution)/shard_map/all_to_all | solution.py:275
  17.0 1.5 collective-permute-start.6
  18.5 2.4 %collective-permute-start.13 = (bf16[288,128]{1,0:T(8,128)(2,1)S(1)}, bf16[288,128]{1,0:T(8,128)(2,1)S(1)}, u32[]{:S(2)}, u32[]{:S(2)}) collective-permute-start(bf16[288,128]{1,0:T(8,128)(2,1)S(1)} %get-tuple-element.31), channel_id=1, source_target_pairs={{0,1},{1,0},{2,3},{3,2},{4,5},{5,4},{6,7},{7,6},{8,9},{9,8},{10,11... | collective-permute-start | bytes 221192 | tf_op jit(solution)/shard_map/ppermute | solution.py:284
  20.9 1.0 collective-permute-start.10
  21.9 6.9 %collective-permute-done.6.refs_5_ = bf16[4,144,128]{2,1,0:T(8,128)(2,1)S(1)} collective-permute-done((bf16[4,144,128]{2,1,0:T(8,128)(2,1)S(1)}, bf16[4,144,128]{2,1,0:T(8,128)(2,1)S(1)}, u32[]{:S(2)}, u32[]{:S(2)}) %collective-permute-start.6) | collective-permute-done | bytes 147488 | tf_op jit(solution)/shard_map/ppermute | solution.py:280
  29.4 1.3 collective-permute-start.14
  30.7 2.1 %collective-permute-start.11 = (bf16[4,144,128]{2,1,0:T(8,128)(2,1)S(1)}, bf16[4,144,128]{2,1,0:T(8,128)(2,1)S(1)}, u32[]{:S(2)}, u32[]{:S(2)}) collective-permute-start(bf16[4,144,128]{2,1,0:T(8,128)(2,1)S(1)} %collective-permute-done.10.refs_11_), channel_id=1, source_target_pairs={{0,56},{8,0},{16,8},{24,16},{32,24},{40,32},{48,40},{56,48},{1,57}... | collective-permute-start | bytes 442376 | tf_op jit(solution)/shard_map/ppermute | solution.py:280
  32.9 2.1 %collective-permute-start.2 = (bf16[8,144,128]{2,1,0:T(8,128)(2,1)S(1)}, bf16[8,144,128]{2,1,0:T(8,128)(2,1)S(1)}, u32[]{:S(2)}, u32[]{:S(2)}) collective-permute-start(bf16[8,144,128]{2,1,0:T(8,128)(2,1)S(1)} %all-to-all-done.refs_0_), channel_id=1, source_target_pairs={{0,192},{64,0},{128,64},{192,128},{1,193},{65,1},{129,65},{193,129... | collective-permute-start | bytes 884744 | tf_op jit(solution)/shard_map/ppermute | solution.py:280
  35.0 1.3 collective-permute-start.1
  36.7 3.0 %collective-permute-start.15 = (bf16[4,288,128]{2,1,0:T(8,128)(2,1)S(1)}, bf16[4,288,128]{2,1,0:T(8,128)(2,1)S(1)}, u32[]{:S(2)}, u32[]{:S(2)}) collective-permute-start(bf16[4,288,128]{2,1,0:T(8,128)(2,1)S(1)} %pad_maximum_fusion.refs_12_), channel_id=1, source_target_pairs={{0,4},{2,6},{4,0},{6,2},{1,5},{3,7},{5,1},{7,3},{8,12},{10,14},{12... | collective-permute-start | bytes 884744 | tf_op jit(solution)/shard_map/ppermute | solution.py:284
  40.2 2.2 %collective-permute-start.12 = (bf16[4,144,128]{2,1,0:T(8,128)(2,1)S(1)}, bf16[4,144,128]{2,1,0:T(8,128)(2,1)S(1)}, u32[]{:S(2)}, u32[]{:S(2)}) collective-permute-start(bf16[4,144,128]{2,1,0:T(8,128)(2,1)S(1)} %collective-permute-done.11.refs_10_), channel_id=1, source_target_pairs={{0,56},{8,0},{16,8},{24,16},{32,24},{40,32},{48,40},{56,48},{1,57}... | collective-permute-start | bytes 442376 | tf_op jit(solution)/shard_map/ppermute | solution.py:280
  42.5 8.6 %collective-permute-done.refs_1_ = bf16[8,144,128]{2,1,0:T(8,128)(2,1)S(1)} collective-permute-done((bf16[8,144,128]{2,1,0:T(8,128)(2,1)S(1)}, bf16[8,144,128]{2,1,0:T(8,128)(2,1)S(1)}, u32[]{:S(2)}, u32[]{:S(2)}) %collective-permute-start) | collective-permute-done | bytes 294944 | tf_op jit(solution)/shard_map/ppermute | solution.py:280
  51.9 37.1 %attend.2 = (bf16[4,288,128]{2,1,0:T(8,128)(2,1)S(1)}, bf16[4,288,128]{2,1,0:T(8,128)(2,1)S(1)}) custom-call(s32[4]{0:T(128)} %pad_add_fusion.at_ref, s32[1,16]{1,0:T(1,128)} %pairs_ref.5, s32[1]{0:T(128)S(6)} %copy.32.counts_ref, s32[32]{0:T(128)} %owner_ref.5, s32[32]{0:T(128)} %convert_reduce_fusion.named_ref, bf16[8,144,128]{2,1,0:T(8,128)(2,1)} %copy-done, ...), custom_call_target="tpu_custom_call" | custom-call | tf_op jit(solution)/shard_map/attend/pallas_call | solution.py:354
  89.1 3.1 %collective-permute-start.16 = (bf16[4,288,128]{2,1,0:T(8,128)(2,1)S(1)}, bf16[4,288,128]{2,1,0:T(8,128)(2,1)S(1)}, u32[]{:S(2)}, u32[]{:S(2)}) collective-permute-start(bf16[4,288,128]{2,1,0:T(8,128)(2,1)S(1)} %get-tuple-element.33), channel_id=1, source_target_pairs={{0,1},{1,0},{2,3},{3,2},{4,5},{5,4},{6,7},{7,6},{8,9},{9,8},{10,11... | collective-permute-start | bytes 884744 | tf_op jit(solution)/shard_map/ppermute | solution.py:280
  92.2 1.2 collective-permute-done.16.other_ref
  94.0 2.9 %collective-permute-start.18 = (bf16[288,128]{1,0:T(8,128)(2,1)S(1)}, bf16[288,128]{1,0:T(8,128)(2,1)S(1)}, u32[]{:S(2)}, u32[]{:S(2)}) collective-permute-start(bf16[288,128]{1,0:T(8,128)(2,1)S(1)} %get-tuple-element.36), channel_id=1, source_target_pairs={{0,4},{2,6},{4,0},{6,2},{1,5},{3,7},{5,1},{7,3},{8,12},{10,14},{12... | collective-permute-start | bytes 221192 | tf_op jit(solution)/shard_map/ppermute | solution.py:284
  97.7 1.5 dynamic-slice_bitcast_fusion.refs_5_
  100.2 1.6 collective-permute-done.19.refs_3_
  101.8 2.3 %settle.2 = (f32[128,128]{1,0:T(8,128)S(1)}, f32[1,128]{1,0:T(1,128)}, f32[136,128]{1,0:T(8,128)S(1)}, bf16[288,128]{1,0:T(8,128)(2,1)S(1)}, bf16[8,144,128]{2,1,0:T(8,128)(2,1)}, /*index=5*/bf16[144,128]{1,0:T(8,128)(2,1)S(1)}) custom-call(bf16[288,128]{1,0:T(8,128)(2,1)S(1)} %get-tuple-element.34.refs_0_, ...), custom_call_target="tpu_custom_call" | custom-call | tf_op jit(solution)/shard_map/settle/pallas_call | solution.py:386
  104.1 1.5 collective-permute-start.23
  105.6 1.3 collective-permute-done.25
  106.9 1.5 collective-permute-done.24
  109.4 18.9 %all-to-all-start.1 = ((bf16[8,144,128]{2,1,0:T(8,128)(2,1)}), bf16[8,144,128]{2,1,0:T(8,128)(2,1)S(1)}, u32[]{:S(2)}, u32[]{:S(2)}) async-start(bf16[8,144,128]{2,1,0:T(8,128)(2,1)} %get-tuple-element.38), calls=%async_computation.1 | async-start | bytes 589824 | tf_op jit(solution)/shard_map/all_to_all | solution.py:275
  128.4 3.6 %collective-permute-start.33 = (bf16[288,128]{1,0:T(8,128)(2,1)S(1)}, bf16[288,128]{1,0:T(8,128)(2,1)S(1)}, u32[]{:S(2)}, u32[]{:S(2)}) collective-permute-start(bf16[288,128]{1,0:T(8,128)(2,1)S(1)} %get-tuple-element.40), channel_id=1, source_target_pairs={{0,1},{1,0},{2,3},{3,2},{4,5},{5,4},{6,7},{7,6},{8,9},{9,8},{10,11... | collective-permute-start | bytes 221192 | tf_op jit(solution)/shard_map/ppermute | solution.py:284
  131.9 1.7 collective-permute-start.26
  133.7 1.3 collective-permute-start.31
  135.1 5.3 %collective-permute-done.26.refs_5_ = bf16[4,144,128]{2,1,0:T(8,128)(2,1)S(1)} collective-permute-done((bf16[4,144,128]{2,1,0:T(8,128)(2,1)S(1)}, bf16[4,144,128]{2,1,0:T(8,128)(2,1)S(1)}, u32[]{:S(2)}, u32[]{:S(2)}) %collective-permute-start.26) | collective-permute-done | bytes 147488 | tf_op jit(solution)/shard_map/ppermute | solution.py:280
  141.1 2.0 %collective-permute-start.32 = (bf16[4,144,128]{2,1,0:T(8,128)(2,1)S(1)}, bf16[4,144,128]{2,1,0:T(8,128)(2,1)S(1)}, u32[]{:S(2)}, u32[]{:S(2)}) collective-permute-start(bf16[4,144,128]{2,1,0:T(8,128)(2,1)S(1)} %collective-permute-done.31.refs_10_), channel_id=1, source_target_pairs={{0,56},{8,0},{16,8},{24,16},{32,24},{40,32},{48,40},{56,48},{1,57}... | collective-permute-start | bytes 442376 | tf_op jit(solution)/shard_map/ppermute | solution.py:280
  144.0 1.6 collective-permute-done.27.refs_6_
  146.3 1.2 collective-permute-start.21
  148.3 2.8 %collective-permute-done.28.refs_7_ = bf16[4,144,128]{2,1,0:T(8,128)(2,1)S(1)} collective-permute-done((bf16[4,144,128]{2,1,0:T(8,128)(2,1)S(1)}, bf16[4,144,128]{2,1,0:T(8,128)(2,1)S(1)}, u32[]{:S(2)}, u32[]{:S(2)}) %collective-permute-start.28) | collective-permute-done | bytes 147488 | tf_op jit(solution)/shard_map/ppermute | solution.py:280
  151.2 5.6 %collective-permute-done.29.refs_8_ = bf16[4,144,128]{2,1,0:T(8,128)(2,1)S(1)} collective-permute-done((bf16[4,144,128]{2,1,0:T(8,128)(2,1)S(1)}, bf16[4,144,128]{2,1,0:T(8,128)(2,1)S(1)}, u32[]{:S(2)}, u32[]{:S(2)}) %collective-permute-start.29) | collective-permute-done | bytes 147488 | tf_op jit(solution)/shard_map/ppermute | solution.py:280
  156.8 4.9 %collective-permute-done.20.refs_1_ = bf16[8,144,128]{2,1,0:T(8,128)(2,1)S(1)} collective-permute-done((bf16[8,144,128]{2,1,0:T(8,128)(2,1)S(1)}, bf16[8,144,128]{2,1,0:T(8,128)(2,1)S(1)}, u32[]{:S(2)}, u32[]{:S(2)}) %collective-permute-start.20) | collective-permute-done | bytes 294944 | tf_op jit(solution)/shard_map/ppermute | solution.py:280
  161.6 8.0 %attend.3 = (bf16[4,288,128]{2,1,0:T(8,128)(2,1)S(1)}, bf16[4,288,128]{2,1,0:T(8,128)(2,1)S(1)}) custom-call(s32[4]{0:T(128)} %pad_add_fusion.at_ref, s32[1,16]{1,0:T(1,128)} %pairs_ref.5, s32[1]{0:T(128)S(6)} %copy.32.counts_ref, s32[32]{0:T(128)} %owner_ref.5, s32[32]{0:T(128)} %convert_reduce_fusion.named_ref, bf16[8,144,128]{2,1,0:T(8,128)(2,1)} %copy-done.1, ...), custom_call_target="tpu_custom_call" | custom-call | tf_op jit(solution)/shard_map/attend/pallas_call | solution.py:354
  169.6 2.1 %collective-permute-start.36 = (bf16[4,288,128]{2,1,0:T(8,128)(2,1)S(1)}, bf16[4,288,128]{2,1,0:T(8,128)(2,1)S(1)}, u32[]{:S(2)}, u32[]{:S(2)}) collective-permute-start(bf16[4,288,128]{2,1,0:T(8,128)(2,1)S(1)} %get-tuple-element.42), channel_id=1, source_target_pairs={{0,1},{1,0},{2,3},{3,2},{4,5},{5,4},{6,7},{7,6},{8,9},{9,8},{10,11... | collective-permute-start | bytes 884744 | tf_op jit(solution)/shard_map/ppermute | solution.py:280
  171.7 1.2 collective-permute-done.36.other_ref
  173.9 2.3 %collective-permute-start.38 = (bf16[288,128]{1,0:T(8,128)(2,1)S(1)}, bf16[288,128]{1,0:T(8,128)(2,1)S(1)}, u32[]{:S(2)}, u32[]{:S(2)}) collective-permute-start(bf16[288,128]{1,0:T(8,128)(2,1)S(1)} %get-tuple-element.45), channel_id=1, source_target_pairs={{0,4},{2,6},{4,0},{6,2},{1,5},{3,7},{5,1},{7,3},{8,12},{10,14},{12... | collective-permute-start | bytes 221192 | tf_op jit(solution)/shard_map/ppermute | solution.py:284
  177.2 2.2 %collective-permute-done.38.refs_2_ = bf16[288,128]{1,0:T(8,128)(2,1)S(1)} collective-permute-done((bf16[288,128]{1,0:T(8,128)(2,1)S(1)}, bf16[288,128]{1,0:T(8,128)(2,1)S(1)}, u32[]{:S(2)}, u32[]{:S(2)}) %collective-permute-start.38) | collective-permute-done | bytes 73760 | tf_op jit(solution)/shard_map/ppermute | solution.py:284
  179.5 1.6 collective-permute-done.39.refs_3_
  181.1 1.1 settle.3
  182.2 1.1 collective-permute-start.42
  183.9 1.5 collective-permute-done.42
  185.4 2.7 %collective-permute-done.41 = f32[136,128]{1,0:T(8,128)S(1)} collective-permute-done((f32[136,128]{1,0:T(8,128)S(1)}, f32[136,128]{1,0:T(8,128)S(1)}, u32[]{:S(2)}, u32[]{:S(2)}) %collective-permute-start.41) | collective-permute-done | bytes 69664 | tf_op jit(solution)/shard_map/ppermute | solution.py:280
  188.6 3.2 %collective-permute-start.43 = (f32[4,136,128]{2,1,0:T(8,128)S(1)}, f32[4,136,128]{2,1,0:T(8,128)S(1)}, u32[]{:S(2)}, u32[]{:S(2)}) collective-permute-start(f32[4,136,128]{2,1,0:T(8,128)S(1)} %pad_maximum_fusion.2.refs_0_), channel_id=1, source_target_pairs={{0,1},{1,0},{2,3},{3,2},{4,5},{5,4},{6,7},{7,6},{8,9},{9,8},{10,11... | collective-permute-start | bytes 835592 | tf_op jit(solution)/shard_map/ppermute | solution.py:280
  191.8 1.2 collective-permute-done.43.refs_1_
  193.0 1.5 finish.1
  (102 shorter events, 13.7 us)
Async XLA Ops:
  4.3 12.6 %collective-permute-start.5 = (bf16[144,128]{1,0:T(8,128)(2,1)S(1)}, bf16[144,128]{1,0:T(8,128)(2,1)S(1)}, u32[]{:S(2)}, u32[]{:S(2)}) collective-permute-start(bf16[144,128]{1,0:T(8,128)(2,1)S(1)} %get-tuple-element.30), channel_id=1, source_target_pairs={{0,192},{64,0},{128,64},{192,128},{1,193},{65,1},{129,65},{193,129... | collective-permute-start | bytes 110600 | tf_op jit(solution)/shard_map/ppermute | solution.py:280
  7.6 9.3 %collective-permute-start.4 = (bf16[144,128]{1,0:T(8,128)(2,1)S(1)}, bf16[144,128]{1,0:T(8,128)(2,1)S(1)}, u32[]{:S(2)}, u32[]{:S(2)}) collective-permute-start(bf16[144,128]{1,0:T(8,128)(2,1)S(1)} %get-tuple-element.30), channel_id=1, source_target_pairs={{0,128},{64,192},{128,0},{192,64},{1,129},{65,193},{129,1},{193,65... | collective-permute-start | bytes 110600 | tf_op jit(solution)/shard_map/ppermute | solution.py:280
  8.2 8.8 %collective-permute-start.3 = (bf16[144,128]{1,0:T(8,128)(2,1)S(1)}, bf16[144,128]{1,0:T(8,128)(2,1)S(1)}, u32[]{:S(2)}, u32[]{:S(2)}) collective-permute-start(bf16[144,128]{1,0:T(8,128)(2,1)S(1)} %get-tuple-element.30), channel_id=1, source_target_pairs={{0,64},{64,128},{128,192},{192,0},{1,65},{65,129},{129,193},{193,1... | collective-permute-start | bytes 110600 | tf_op jit(solution)/shard_map/ppermute | solution.py:280
  8.8 24.1 %all-to-all-start = ((bf16[8,144,128]{2,1,0:T(8,128)(2,1)}), bf16[8,144,128]{2,1,0:T(8,128)(2,1)S(1)}, u32[]{:S(2)}, u32[]{:S(2)}) async-start(bf16[8,144,128]{2,1,0:T(8,128)(2,1)} %get-tuple-element.29), calls=%async_computation | async-start | bytes 589824 | tf_op jit(solution)/shard_map/all_to_all | solution.py:275
  17.0 11.8 %collective-permute-start.6 = (bf16[4,144,128]{2,1,0:T(8,128)(2,1)S(1)}, bf16[4,144,128]{2,1,0:T(8,128)(2,1)S(1)}, u32[]{:S(2)}, u32[]{:S(2)}) collective-permute-start(bf16[4,144,128]{2,1,0:T(8,128)(2,1)S(1)} %pad_maximum_fusion.3.refs_4_), channel_id=1, source_target_pairs={{0,8},{8,16},{16,24},{24,32},{32,40},{40,48},{48,56},{56,0},{1,9},... | collective-permute-start | bytes 442376 | tf_op jit(solution)/shard_map/ppermute | solution.py:280
  18.5 10.3 %collective-permute-start.13 = (bf16[288,128]{1,0:T(8,128)(2,1)S(1)}, bf16[288,128]{1,0:T(8,128)(2,1)S(1)}, u32[]{:S(2)}, u32[]{:S(2)}) collective-permute-start(bf16[288,128]{1,0:T(8,128)(2,1)S(1)} %get-tuple-element.31), channel_id=1, source_target_pairs={{0,1},{1,0},{2,3},{3,2},{4,5},{5,4},{6,7},{7,6},{8,9},{9,8},{10,11... | collective-permute-start | bytes 221192 | tf_op jit(solution)/shard_map/ppermute | solution.py:284
  20.9 9.9 %collective-permute-start.10 = (bf16[4,144,128]{2,1,0:T(8,128)(2,1)S(1)}, bf16[4,144,128]{2,1,0:T(8,128)(2,1)S(1)}, u32[]{:S(2)}, u32[]{:S(2)}) collective-permute-start(bf16[4,144,128]{2,1,0:T(8,128)(2,1)S(1)} %pad_maximum_fusion.3.refs_4_), channel_id=1, source_target_pairs={{0,56},{8,0},{16,8},{24,16},{32,24},{40,32},{48,40},{56,48},{1,57}... | collective-permute-start | bytes 442376 | tf_op jit(solution)/shard_map/ppermute | solution.py:280
  28.8 6.2 %collective-permute-start.7 = (bf16[4,144,128]{2,1,0:T(8,128)(2,1)S(1)}, bf16[4,144,128]{2,1,0:T(8,128)(2,1)S(1)}, u32[]{:S(2)}, u32[]{:S(2)}) collective-permute-start(bf16[4,144,128]{2,1,0:T(8,128)(2,1)S(1)} %collective-permute-done.6.refs_5_), channel_id=1, source_target_pairs={{0,8},{8,16},{16,24},{24,32},{32,40},{40,48},{48,56},{56,0},{1,9},... | collective-permute-start | bytes 442376 | tf_op jit(solution)/shard_map/ppermute | solution.py:280
  29.4 6.9 %collective-permute-start.14 = (bf16[2,288,128]{2,1,0:T(8,128)(2,1)S(1)}, bf16[2,288,128]{2,1,0:T(8,128)(2,1)S(1)}, u32[]{:S(2)}, u32[]{:S(2)}) collective-permute-start(bf16[2,288,128]{2,1,0:T(8,128)(2,1)S(1)} %pad_maximum_fusion.4), channel_id=1, source_target_pairs={{0,2},{2,0},{4,6},{6,4},{1,3},{3,1},{5,7},{7,5},{8,10},{10,8},{12,... | collective-permute-start | bytes 442376 | tf_op jit(solution)/shard_map/ppermute | solution.py:284
  30.7 6.0 %collective-permute-start.11 = (bf16[4,144,128]{2,1,0:T(8,128)(2,1)S(1)}, bf16[4,144,128]{2,1,0:T(8,128)(2,1)S(1)}, u32[]{:S(2)}, u32[]{:S(2)}) collective-permute-start(bf16[4,144,128]{2,1,0:T(8,128)(2,1)S(1)} %collective-permute-done.10.refs_11_), channel_id=1, source_target_pairs={{0,56},{8,0},{16,8},{24,16},{32,24},{40,32},{48,40},{56,48},{1,57}... | collective-permute-start | bytes 442376 | tf_op jit(solution)/shard_map/ppermute | solution.py:280
  32.9 9.5 %collective-permute-start.2 = (bf16[8,144,128]{2,1,0:T(8,128)(2,1)S(1)}, bf16[8,144,128]{2,1,0:T(8,128)(2,1)S(1)}, u32[]{:S(2)}, u32[]{:S(2)}) collective-permute-start(bf16[8,144,128]{2,1,0:T(8,128)(2,1)S(1)} %all-to-all-done.refs_0_), channel_id=1, source_target_pairs={{0,192},{64,0},{128,64},{192,128},{1,193},{65,1},{129,65},{193,129... | collective-permute-start | bytes 884744 | tf_op jit(solution)/shard_map/ppermute | solution.py:280
  35.0 5.2 %collective-permute-start.8 = (bf16[4,144,128]{2,1,0:T(8,128)(2,1)S(1)}, bf16[4,144,128]{2,1,0:T(8,128)(2,1)S(1)}, u32[]{:S(2)}, u32[]{:S(2)}) collective-permute-start(bf16[4,144,128]{2,1,0:T(8,128)(2,1)S(1)} %collective-permute-done.7.refs_6_), channel_id=1, source_target_pairs={{0,8},{8,16},{16,24},{24,32},{32,40},{40,48},{48,56},{56,0},{1,9},... | collective-permute-start | bytes 442376 | tf_op jit(solution)/shard_map/ppermute | solution.py:280
  35.0 7.5 %collective-permute-start.1 = (bf16[8,144,128]{2,1,0:T(8,128)(2,1)S(1)}, bf16[8,144,128]{2,1,0:T(8,128)(2,1)S(1)}, u32[]{:S(2)}, u32[]{:S(2)}) collective-permute-start(bf16[8,144,128]{2,1,0:T(8,128)(2,1)S(1)} %all-to-all-done.refs_0_), channel_id=1, source_target_pairs={{0,128},{64,192},{128,0},{192,64},{1,129},{65,193},{129,1},{193,65... | collective-permute-start | bytes 884744 | tf_op jit(solution)/shard_map/ppermute | solution.py:280
  36.3 14.8 %collective-permute-start = (bf16[8,144,128]{2,1,0:T(8,128)(2,1)S(1)}, bf16[8,144,128]{2,1,0:T(8,128)(2,1)S(1)}, u32[]{:S(2)}, u32[]{:S(2)}) collective-permute-start(bf16[8,144,128]{2,1,0:T(8,128)(2,1)S(1)} %all-to-all-done.refs_0_), channel_id=1, source_target_pairs={{0,64},{64,128},{128,192},{192,0},{1,65},{65,129},{129,193},{193,1... | collective-permute-start | bytes 884744 | tf_op jit(solution)/shard_map/ppermute | solution.py:280
  36.7 15.1 %collective-permute-start.15 = (bf16[4,288,128]{2,1,0:T(8,128)(2,1)S(1)}, bf16[4,288,128]{2,1,0:T(8,128)(2,1)S(1)}, u32[]{:S(2)}, u32[]{:S(2)}) collective-permute-start(bf16[4,288,128]{2,1,0:T(8,128)(2,1)S(1)} %pad_maximum_fusion.refs_12_), channel_id=1, source_target_pairs={{0,4},{2,6},{4,0},{6,2},{1,5},{3,7},{5,1},{7,3},{8,12},{10,14},{12... | collective-permute-start | bytes 884744 | tf_op jit(solution)/shard_map/ppermute | solution.py:284
  40.2 11.7 %collective-permute-start.12 = (bf16[4,144,128]{2,1,0:T(8,128)(2,1)S(1)}, bf16[4,144,128]{2,1,0:T(8,128)(2,1)S(1)}, u32[]{:S(2)}, u32[]{:S(2)}) collective-permute-start(bf16[4,144,128]{2,1,0:T(8,128)(2,1)S(1)} %collective-permute-done.11.refs_10_), channel_id=1, source_target_pairs={{0,56},{8,0},{16,8},{24,16},{32,24},{40,32},{48,40},{56,48},{1,57}... | collective-permute-start | bytes 442376 | tf_op jit(solution)/shard_map/ppermute | solution.py:280
  42.4 9.5 %collective-permute-start.9 = (bf16[4,144,128]{2,1,0:T(8,128)(2,1)S(1)}, bf16[4,144,128]{2,1,0:T(8,128)(2,1)S(1)}, u32[]{:S(2)}, u32[]{:S(2)}) collective-permute-start(bf16[4,144,128]{2,1,0:T(8,128)(2,1)S(1)} %collective-permute-done.8.refs_7_), channel_id=1, source_target_pairs={{0,8},{8,16},{16,24},{24,32},{32,40},{40,48},{48,56},{56,0},{1,9},... | collective-permute-start | bytes 442376 | tf_op jit(solution)/shard_map/ppermute | solution.py:280
  89.1 4.3 %collective-permute-start.16 = (bf16[4,288,128]{2,1,0:T(8,128)(2,1)S(1)}, bf16[4,288,128]{2,1,0:T(8,128)(2,1)S(1)}, u32[]{:S(2)}, u32[]{:S(2)}) collective-permute-start(bf16[4,288,128]{2,1,0:T(8,128)(2,1)S(1)} %get-tuple-element.33), channel_id=1, source_target_pairs={{0,1},{1,0},{2,3},{3,2},{4,5},{5,4},{6,7},{7,6},{8,9},{9,8},{10,11... | collective-permute-start | bytes 884744 | tf_op jit(solution)/shard_map/ppermute | solution.py:280
  93.7 5.4 %collective-permute-start.17 = (bf16[288,128]{1,0:T(8,128)(2,1)S(1)}, bf16[288,128]{1,0:T(8,128)(2,1)S(1)}, u32[]{:S(2)}, u32[]{:S(2)}) collective-permute-start(bf16[288,128]{1,0:T(8,128)(2,1)S(1)} %get-tuple-element.35), channel_id=1, source_target_pairs={{0,2},{2,0},{4,6},{6,4},{1,3},{3,1},{5,7},{7,5},{8,10},{10,8},{12,... | collective-permute-start | bytes 221192 | tf_op jit(solution)/shard_map/ppermute | solution.py:284
  94.0 6.2 %collective-permute-start.18 = (bf16[288,128]{1,0:T(8,128)(2,1)S(1)}, bf16[288,128]{1,0:T(8,128)(2,1)S(1)}, u32[]{:S(2)}, u32[]{:S(2)}) collective-permute-start(bf16[288,128]{1,0:T(8,128)(2,1)S(1)} %get-tuple-element.36), channel_id=1, source_target_pairs={{0,4},{2,6},{4,0},{6,2},{1,5},{3,7},{5,1},{7,3},{8,12},{10,14},{12... | collective-permute-start | bytes 221192 | tf_op jit(solution)/shard_map/ppermute | solution.py:284
  96.9 4.9 %collective-permute-start.19 = (bf16[288,128]{1,0:T(8,128)(2,1)S(1)}, bf16[288,128]{1,0:T(8,128)(2,1)S(1)}, u32[]{:S(2)}, u32[]{:S(2)}) collective-permute-start(bf16[288,128]{1,0:T(8,128)(2,1)S(1)} %get-tuple-element.37), channel_id=1, source_target_pairs={{0,6},{2,4},{4,2},{6,0},{1,7},{3,5},{5,3},{7,1},{8,14},{10,12},{12... | collective-permute-start | bytes 221192 | tf_op jit(solution)/shard_map/ppermute | solution.py:284
  104.1 2.8 %collective-permute-start.25 = (bf16[144,128]{1,0:T(8,128)(2,1)S(1)}, bf16[144,128]{1,0:T(8,128)(2,1)S(1)}, u32[]{:S(2)}, u32[]{:S(2)}) collective-permute-start(bf16[144,128]{1,0:T(8,128)(2,1)S(1)} %get-tuple-element.39), channel_id=1, source_target_pairs={{0,192},{64,0},{128,64},{192,128},{1,193},{65,1},{129,65},{193,129... | collective-permute-start | bytes 110600 | tf_op jit(solution)/shard_map/ppermute | solution.py:280
  104.1 4.3 %collective-permute-start.24 = (bf16[144,128]{1,0:T(8,128)(2,1)S(1)}, bf16[144,128]{1,0:T(8,128)(2,1)S(1)}, u32[]{:S(2)}, u32[]{:S(2)}) collective-permute-start(bf16[144,128]{1,0:T(8,128)(2,1)S(1)} %get-tuple-element.39), channel_id=1, source_target_pairs={{0,128},{64,192},{128,0},{192,64},{1,129},{65,193},{129,1},{193,65... | collective-permute-start | bytes 110600 | tf_op jit(solution)/shard_map/ppermute | solution.py:280
  104.1 5.2 %collective-permute-start.23 = (bf16[144,128]{1,0:T(8,128)(2,1)S(1)}, bf16[144,128]{1,0:T(8,128)(2,1)S(1)}, u32[]{:S(2)}, u32[]{:S(2)}) collective-permute-start(bf16[144,128]{1,0:T(8,128)(2,1)S(1)} %get-tuple-element.39), channel_id=1, source_target_pairs={{0,64},{64,128},{128,192},{192,0},{1,65},{65,129},{129,193},{193,1... | collective-permute-start | bytes 110600 | tf_op jit(solution)/shard_map/ppermute | solution.py:280
  109.3 22.6 %copy-start.5 = (bf16[4,144,128]{2,1,0:T(8,128)(2,1)}, bf16[4,144,128]{2,1,0:T(8,128)(2,1)S(1)}, u32[]{:S(2)}) copy-start(bf16[4,144,128]{2,1,0:T(8,128)(2,1)S(1)} %pad_maximum_fusion.5.refs_4_) | copy-start | bytes 442372
  109.3 24.4 %collective-permute-start.30 = (bf16[4,144,128]{2,1,0:T(8,128)(2,1)S(1)}, bf16[4,144,128]{2,1,0:T(8,128)(2,1)S(1)}, u32[]{:S(2)}, u32[]{:S(2)}) collective-permute-start(bf16[4,144,128]{2,1,0:T(8,128)(2,1)S(1)} %pad_maximum_fusion.5.refs_4_), channel_id=1, source_target_pairs={{0,56},{8,0},{16,8},{24,16},{32,24},{40,32},{48,40},{56,48},{1,57}... | collective-permute-start | bytes 442376 | tf_op jit(solution)/shard_map/ppermute | solution.py:280
  109.4 36.3 %all-to-all-start.1 = ((bf16[8,144,128]{2,1,0:T(8,128)(2,1)}), bf16[8,144,128]{2,1,0:T(8,128)(2,1)S(1)}, u32[]{:S(2)}, u32[]{:S(2)}) async-start(bf16[8,144,128]{2,1,0:T(8,128)(2,1)} %get-tuple-element.38), calls=%async_computation.1 | async-start | bytes 589824 | tf_op jit(solution)/shard_map/all_to_all | solution.py:275
  128.4 6.6 %collective-permute-start.33 = (bf16[288,128]{1,0:T(8,128)(2,1)S(1)}, bf16[288,128]{1,0:T(8,128)(2,1)S(1)}, u32[]{:S(2)}, u32[]{:S(2)}) collective-permute-start(bf16[288,128]{1,0:T(8,128)(2,1)S(1)} %get-tuple-element.40), channel_id=1, source_target_pairs={{0,1},{1,0},{2,3},{3,2},{4,5},{5,4},{6,7},{7,6},{8,9},{9,8},{10,11... | collective-permute-start | bytes 221192 | tf_op jit(solution)/shard_map/ppermute | solution.py:284
  131.9 8.5 %collective-permute-start.26 = (bf16[4,144,128]{2,1,0:T(8,128)(2,1)S(1)}, bf16[4,144,128]{2,1,0:T(8,128)(2,1)S(1)}, u32[]{:S(2)}, u32[]{:S(2)}) collective-permute-start(bf16[4,144,128]{2,1,0:T(8,128)(2,1)S(1)} %pad_maximum_fusion.5.refs_4_), channel_id=1, source_target_pairs={{0,8},{8,16},{16,24},{24,32},{32,40},{40,48},{48,56},{56,0},{1,9},... | collective-permute-start | bytes 442376 | tf_op jit(solution)/shard_map/ppermute | solution.py:280
  133.7 7.4 %collective-permute-start.31 = (bf16[4,144,128]{2,1,0:T(8,128)(2,1)S(1)}, bf16[4,144,128]{2,1,0:T(8,128)(2,1)S(1)}, u32[]{:S(2)}, u32[]{:S(2)}) collective-permute-start(bf16[4,144,128]{2,1,0:T(8,128)(2,1)S(1)} %collective-permute-done.30.refs_11_), channel_id=1, source_target_pairs={{0,56},{8,0},{16,8},{24,16},{32,24},{40,32},{48,40},{56,48},{1,57}... | collective-permute-start | bytes 442376 | tf_op jit(solution)/shard_map/ppermute | solution.py:280
  135.0 8.1 %collective-permute-start.34 = (bf16[2,288,128]{2,1,0:T(8,128)(2,1)S(1)}, bf16[2,288,128]{2,1,0:T(8,128)(2,1)S(1)}, u32[]{:S(2)}, u32[]{:S(2)}) collective-permute-start(bf16[2,288,128]{2,1,0:T(8,128)(2,1)S(1)} %pad_maximum_fusion.6), channel_id=1, source_target_pairs={{0,2},{2,0},{4,6},{6,4},{1,3},{3,1},{5,7},{7,5},{8,10},{10,8},{12,... | collective-permute-start | bytes 442376 | tf_op jit(solution)/shard_map/ppermute | solution.py:284
  140.5 5.2 %collective-permute-start.27 = (bf16[4,144,128]{2,1,0:T(8,128)(2,1)S(1)}, bf16[4,144,128]{2,1,0:T(8,128)(2,1)S(1)}, u32[]{:S(2)}, u32[]{:S(2)}) collective-permute-start(bf16[4,144,128]{2,1,0:T(8,128)(2,1)S(1)} %collective-permute-done.26.refs_5_), channel_id=1, source_target_pairs={{0,8},{8,16},{16,24},{24,32},{32,40},{40,48},{48,56},{56,0},{1,9},... | collective-permute-start | bytes 442376 | tf_op jit(solution)/shard_map/ppermute | solution.py:280
  141.1 6.4 %collective-permute-start.32 = (bf16[4,144,128]{2,1,0:T(8,128)(2,1)S(1)}, bf16[4,144,128]{2,1,0:T(8,128)(2,1)S(1)}, u32[]{:S(2)}, u32[]{:S(2)}) collective-permute-start(bf16[4,144,128]{2,1,0:T(8,128)(2,1)S(1)} %collective-permute-done.31.refs_10_), channel_id=1, source_target_pairs={{0,56},{8,0},{16,8},{24,16},{32,24},{40,32},{48,40},{56,48},{1,57}... | collective-permute-start | bytes 442376 | tf_op jit(solution)/shard_map/ppermute | solution.py:280
  143.2 18.4 %copy-start.3 = (bf16[4,288,128]{2,1,0:T(8,128)(2,1)}, bf16[4,288,128]{2,1,0:T(8,128)(2,1)S(1)}, u32[]{:S(2)}) copy-start(bf16[4,288,128]{2,1,0:T(8,128)(2,1)S(1)} %pad_maximum_fusion.1.refs_12_) | copy-start | bytes 884740
  143.2 8.0 %collective-permute-start.35 = (bf16[4,288,128]{2,1,0:T(8,128)(2,1)S(1)}, bf16[4,288,128]{2,1,0:T(8,128)(2,1)S(1)}, u32[]{:S(2)}, u32[]{:S(2)}) collective-permute-start(bf16[4,288,128]{2,1,0:T(8,128)(2,1)S(1)} %pad_maximum_fusion.1.refs_12_), channel_id=1, source_target_pairs={{0,4},{2,6},{4,0},{6,2},{1,5},{3,7},{5,1},{7,3},{8,12},{10,14},{12... | collective-permute-start | bytes 884744 | tf_op jit(solution)/shard_map/ppermute | solution.py:284
  145.7 5.5 %collective-permute-start.28 = (bf16[4,144,128]{2,1,0:T(8,128)(2,1)S(1)}, bf16[4,144,128]{2,1,0:T(8,128)(2,1)S(1)}, u32[]{:S(2)}, u32[]{:S(2)}) collective-permute-start(bf16[4,144,128]{2,1,0:T(8,128)(2,1)S(1)} %collective-permute-done.27.refs_6_), channel_id=1, source_target_pairs={{0,8},{8,16},{16,24},{24,32},{32,40},{40,48},{48,56},{56,0},{1,9},... | collective-permute-start | bytes 442376 | tf_op jit(solution)/shard_map/ppermute | solution.py:280
  145.7 11.1 %collective-permute-start.22 = (bf16[8,144,128]{2,1,0:T(8,128)(2,1)S(1)}, bf16[8,144,128]{2,1,0:T(8,128)(2,1)S(1)}, u32[]{:S(2)}, u32[]{:S(2)}) collective-permute-start(bf16[8,144,128]{2,1,0:T(8,128)(2,1)S(1)} %all-to-all-done.1.refs_0_), channel_id=1, source_target_pairs={{0,192},{64,0},{128,64},{192,128},{1,193},{65,1},{129,65},{193,129... | collective-permute-start | bytes 884744 | tf_op jit(solution)/shard_map/ppermute | solution.py:280
  146.3 10.4 %collective-permute-start.21 = (bf16[8,144,128]{2,1,0:T(8,128)(2,1)S(1)}, bf16[8,144,128]{2,1,0:T(8,128)(2,1)S(1)}, u32[]{:S(2)}, u32[]{:S(2)}) collective-permute-start(bf16[8,144,128]{2,1,0:T(8,128)(2,1)S(1)} %all-to-all-done.1.refs_0_), channel_id=1, source_target_pairs={{0,128},{64,192},{128,0},{192,64},{1,129},{65,193},{129,1},{193,65... | collective-permute-start | bytes 884744 | tf_op jit(solution)/shard_map/ppermute | solution.py:280
  147.6 14.1 %collective-permute-start.20 = (bf16[8,144,128]{2,1,0:T(8,128)(2,1)S(1)}, bf16[8,144,128]{2,1,0:T(8,128)(2,1)S(1)}, u32[]{:S(2)}, u32[]{:S(2)}) collective-permute-start(bf16[8,144,128]{2,1,0:T(8,128)(2,1)S(1)} %all-to-all-done.1.refs_0_), channel_id=1, source_target_pairs={{0,64},{64,128},{128,192},{192,0},{1,65},{65,129},{129,193},{193,1... | collective-permute-start | bytes 884744 | tf_op jit(solution)/shard_map/ppermute | solution.py:280
  151.2 5.6 %collective-permute-start.29 = (bf16[4,144,128]{2,1,0:T(8,128)(2,1)S(1)}, bf16[4,144,128]{2,1,0:T(8,128)(2,1)S(1)}, u32[]{:S(2)}, u32[]{:S(2)}) collective-permute-start(bf16[4,144,128]{2,1,0:T(8,128)(2,1)S(1)} %collective-permute-done.28.refs_7_), channel_id=1, source_target_pairs={{0,8},{8,16},{16,24},{24,32},{32,40},{40,48},{48,56},{56,0},{1,9},... | collective-permute-start | bytes 442376 | tf_op jit(solution)/shard_map/ppermute | solution.py:280
  169.6 3.3 %collective-permute-start.36 = (bf16[4,288,128]{2,1,0:T(8,128)(2,1)S(1)}, bf16[4,288,128]{2,1,0:T(8,128)(2,1)S(1)}, u32[]{:S(2)}, u32[]{:S(2)}) collective-permute-start(bf16[4,288,128]{2,1,0:T(8,128)(2,1)S(1)} %get-tuple-element.42), channel_id=1, source_target_pairs={{0,1},{1,0},{2,3},{3,2},{4,5},{5,4},{6,7},{7,6},{8,9},{9,8},{10,11... | collective-permute-start | bytes 884744 | tf_op jit(solution)/shard_map/ppermute | solution.py:280
  173.3 3.9 %collective-permute-start.37 = (bf16[288,128]{1,0:T(8,128)(2,1)S(1)}, bf16[288,128]{1,0:T(8,128)(2,1)S(1)}, u32[]{:S(2)}, u32[]{:S(2)}) collective-permute-start(bf16[288,128]{1,0:T(8,128)(2,1)S(1)} %get-tuple-element.44), channel_id=1, source_target_pairs={{0,2},{2,0},{4,6},{6,4},{1,3},{3,1},{5,7},{7,5},{8,10},{10,8},{12,... | collective-permute-start | bytes 221192 | tf_op jit(solution)/shard_map/ppermute | solution.py:284
  173.9 5.6 %collective-permute-start.38 = (bf16[288,128]{1,0:T(8,128)(2,1)S(1)}, bf16[288,128]{1,0:T(8,128)(2,1)S(1)}, u32[]{:S(2)}, u32[]{:S(2)}) collective-permute-start(bf16[288,128]{1,0:T(8,128)(2,1)S(1)} %get-tuple-element.45), channel_id=1, source_target_pairs={{0,4},{2,6},{4,0},{6,2},{1,5},{3,7},{5,1},{7,3},{8,12},{10,14},{12... | collective-permute-start | bytes 221192 | tf_op jit(solution)/shard_map/ppermute | solution.py:284
  176.2 4.9 %collective-permute-start.39 = (bf16[288,128]{1,0:T(8,128)(2,1)S(1)}, bf16[288,128]{1,0:T(8,128)(2,1)S(1)}, u32[]{:S(2)}, u32[]{:S(2)}) collective-permute-start(bf16[288,128]{1,0:T(8,128)(2,1)S(1)} %get-tuple-element.46), channel_id=1, source_target_pairs={{0,6},{2,4},{4,2},{6,0},{1,7},{3,5},{5,3},{7,1},{8,14},{10,12},{12... | collective-permute-start | bytes 221192 | tf_op jit(solution)/shard_map/ppermute | solution.py:284
  182.2 3.2 %collective-permute-start.42 = (f32[136,128]{1,0:T(8,128)S(1)}, f32[136,128]{1,0:T(8,128)S(1)}, u32[]{:S(2)}, u32[]{:S(2)}) collective-permute-start(f32[136,128]{1,0:T(8,128)S(1)} %get-tuple-element.49), channel_id=1, source_target_pairs={{0,6},{2,0},{4,2},{6,4},{1,7},{3,1},{5,3},{7,5},{8,14},{10,8},{12,... | collective-permute-start | bytes 208904 | tf_op jit(solution)/shard_map/ppermute | solution.py:280
  183.3 4.8 %collective-permute-start.41 = (f32[136,128]{1,0:T(8,128)S(1)}, f32[136,128]{1,0:T(8,128)S(1)}, u32[]{:S(2)}, u32[]{:S(2)}) collective-permute-start(f32[136,128]{1,0:T(8,128)S(1)} %get-tuple-element.49), channel_id=1, source_target_pairs={{0,4},{2,6},{4,0},{6,2},{1,5},{3,7},{5,1},{7,3},{8,12},{10,14},{12... | collective-permute-start | bytes 208904 | tf_op jit(solution)/shard_map/ppermute | solution.py:280
  183.3 5.2 %collective-permute-start.40 = (f32[136,128]{1,0:T(8,128)S(1)}, f32[136,128]{1,0:T(8,128)S(1)}, u32[]{:S(2)}, u32[]{:S(2)}) collective-permute-start(f32[136,128]{1,0:T(8,128)S(1)} %get-tuple-element.49), channel_id=1, source_target_pairs={{0,2},{2,4},{4,6},{6,0},{1,3},{3,5},{5,7},{7,1},{8,10},{10,12},{12... | collective-permute-start | bytes 208904 | tf_op jit(solution)/shard_map/ppermute | solution.py:280
  188.6 4.4 %collective-permute-start.43 = (f32[4,136,128]{2,1,0:T(8,128)S(1)}, f32[4,136,128]{2,1,0:T(8,128)S(1)}, u32[]{:S(2)}, u32[]{:S(2)}) collective-permute-start(f32[4,136,128]{2,1,0:T(8,128)S(1)} %pad_maximum_fusion.2.refs_0_), channel_id=1, source_target_pairs={{0,1},{1,0},{2,3},{3,2},{4,5},{5,4},{6,7},{7,6},{8,9},{9,8},{10,11... | collective-permute-start | bytes 835592 | tf_op jit(solution)/shard_map/ppermute | solution.py:280
  (14 other events, 120.2 us)
where the time goes:
time: 195 us; the launch traced here: 194 us
  starting transfers between devices  81.2 us (42%)
  waiting for transfers between devices  54.7 us (28%)
  Pallas kernels  53.2 us (27%)
  local copies, waits for them, and re-layouts  2.19 us (1%)
    ppermute x32, waiting for transfers between devices, shifted(): return lax.ppermute(x, axis, [(i, (i + step) % n) for i in range(n)])  48.2 us
    pallas_call x2, Pallas kernels, on_device(): pl.pallas_call(attend_kernel, out_shape=(half_shape, half_shape), in_spec...  45.1 us
    ppermute x32, starting transfers between devices, shifted(): return lax.ppermute(x, axis, [(i, (i + step) % n) for i in range(n)])  35 us
    all_to_all x2, starting transfers between devices, exchanged(): return lax.all_to_all(copies, axes, split_axis=0, concat_axis=0, tiled=True)  27.1 us
    ppermute x12, starting transfers between devices, crossed(): lax.ppermute(x, axis, [(i, i ^ bit) for i in range(lax.axis_size(axis))])  19.1 us
    ppermute x12, waiting for transfers between devices, crossed(): lax.ppermute(x, axis, [(i, i ^ bit) for i in range(lax.axis_size(axis))])  6.54 us
  transfers between devices with their start and end apart: 46, of which 21 were waited for; matrix products, arithmetic and copies ran while one was open for 1% of the time, Pallas kernels for 0%

commit v1 on v0

--- a/solution.py
+++ b/solution.py
@@ -16,6 +16,7 @@
 MSG = 2 * SIDE
 META = 8
 SQUARE = 9
+GROUP = 4
 LIMIT = 40.0
 XS, ZS, YS, CS = 4, 8, 4, 2
 TEMPER = 0.25
@@ -121,40 +122,36 @@
     def one_side(side, carry):
         q_at = pl.multiple_of(side * SIDE, 16)
         live = jnp.where(side == 0, naming, counts_ref[0])
-        list_ref[side, live] = list_ref[side, 0]
+        for n in range(GROUP - 1):
+            list_ref[side, live + n] = list_ref[side, 0]
         for c in range(helpers):
             scaled_ref[pl.ds(c * SHARD, SHARD), :] = query_refs[c][pl.ds(q_at, SHARD), :] * jnp.asarray(
                 2.0 / (WIDTH * TEMPER), BF16
             )
         sum_ref[...] = jnp.zeros(sum_ref.shape, F32)
         acc_ref[...] = jnp.zeros(acc_ref.shape, F32)
-        turns = (live + 1) // 2
+        turns = (live + GROUP - 1) // GROUP
 
         def biases(t):
-            left = of_three(key_ref[list_ref[side, 2 * t], pl.ds(SHARD, 16), :])
-            right = of_three(key_ref[list_ref[side, 2 * t + 1], pl.ds(SHARD, 16), :])
-            return left, jnp.where(2 * t + 1 < live, right, LOW)
+            rows = [of_three(key_ref[list_ref[side, GROUP * t + n], pl.ds(SHARD, 16), :]) for n in range(GROUP)]
+            return [jnp.where(GROUP * t + n < live, row, LOW) for n, row in enumerate(rows)]
 
         def scores(t, shift, rows):
-            first = key_ref[list_ref[side, 2 * t], pl.ds(0, SHARD), :]
-            second = key_ref[list_ref[side, 2 * t + 1], pl.ds(0, SHARD), :]
-            key = jnp.concatenate([first, second], axis=0)
-            left, right = biases(t)
+            key = jnp.concatenate([key_ref[list_ref[side, GROUP * t + n], pl.ds(0, SHARD), :] for n in range(GROUP)])
             cross = lax.dot_general(scaled_ref[rows, :], key, LANES, preferred_element_type=F32)
-            return cross[:, :SHARD] + (left - shift), cross[:, SHARD:] + (right - shift), key
-
-        def add(left, right, key, rows):
-            left = jnp.exp(left)
-            right = jnp.exp(right)
-            sum_ref[rows, :] += left + right
-            weight = jnp.concatenate([left.astype(BF16), right.astype(BF16)], axis=1)
+            parts = [cross[:, n * SHARD : (n + 1) * SHARD] + (row - shift) for n, row in enumerate(biases(t))]
+            return parts, key
+
+        def add(parts, key, rows):
+            parts = [jnp.exp(part) for part in parts]
+            sum_ref[rows, :] += functools.reduce(jnp.add, parts)
+            weight = jnp.concatenate([part.astype(BF16) for part in parts], axis=1)
             acc_ref[rows, :] += jnp.dot(weight, key, preferred_element_type=F32)
 
         @pl.when(safe)
         def _():
             def top_bias(t, top):
-                left, right = biases(t)
-                return jnp.maximum(top, jnp.maximum(left, right))
+                return functools.reduce(jnp.maximum, biases(t), top)
 
             top = lax.fori_loop(0, turns, top_bias, jnp.full((1, WIDTH), LOW, F32))
             top = jnp.max(top, axis=1, keepdims=True)
@@ -173,16 +170,15 @@
                 rows = pl.ds(pl.multiple_of(c * SHARD, SHARD), SHARD)
 
                 def find_peak(t, peak):
-                    left, right, _ = scores(t, 0.0, rows)
-                    return jnp.maximum(peak, jnp.maximum(left, right))
+                    return functools.reduce(jnp.maximum, scores(t, 0.0, rows)[0], peak)
 
                 peak = lax.fori_loop(0, turns, find_peak, jnp.full((SHARD, WIDTH), LOW, F32))
                 top = jnp.broadcast_to(jnp.max(peak, axis=1, keepdims=True), (SHARD, WIDTH))
                 shift_ref[:, rows] = top.T[:16]
 
                 def add_up(t, carry):
-                    left, right, key = scores(t, 0.0, rows)
-                    add(left - top, right - top, key, rows)
+                    parts, key = scores(t, 0.0, rows)
+                    add([part - top for part in parts], key, rows)
                     return carry
 
                 return lax.fori_loop(0, turns, add_up, carry)
@@ -357,7 +353,7 @@
             in_specs=[smem] * 5 + [vmem] * (XS + ZS + 2),
             out_specs=(vmem, vmem),
             scratch_shapes=[
-                pltpu.SMEM((2, blocks + 1), jnp.int32),
+                pltpu.SMEM((2, blocks + GROUP), jnp.int32),
                 pltpu.VMEM((2 * blocks, SIDE, WIDTH), BF16),
                 pltpu.VMEM((helpers * SHARD, WIDTH), BF16),
                 pltpu.VMEM((16, helpers * SHARD), F32),

time: 195 us -> 177 us (0.908)
  Pallas kernels: 53.2 us -> 38.1 us
  starting transfers between devices: 81.2 us -> 78.3 us
    pallas_call x2, Pallas kernels: 45.1 us -> 30 us  [on_device(): pl.pallas_call(attend_kernel, out_shape=(half_shape, half_shape), in_spec...]
    all_to_all x2, starting transfers between devices: 27.1 us -> 23.2 us  [exchanged(): return lax.all_to_all(copies, axes, split_axis=0, concat_axis=0, tiled=True)]
where the time goes in v1:
time: 177 us; the launch traced here: 176 us
  starting transfers between devices  78.3 us (44%)
  waiting for transfers between devices  54.7 us (31%)
  Pallas kernels  38.1 us (22%)
  local copies, waits for them, and re-layouts  2.19 us (1%)
    ppermute x32, waiting for transfers between devices, shifted(): return lax.ppermute(x, axis, [(i, (i + step) % n) for i in range(n)])  48.2 us
    ppermute x32, starting transfers between devices, shifted(): return lax.ppermute(x, axis, [(i, (i + step) % n) for i in range(n)])  36.1 us
    pallas_call x2, Pallas kernels, on_device(): pl.pallas_call(attend_kernel, out_shape=(half_shape, half_shape), in_spec...  30 us
    all_to_all x2, starting transfers between devices, exchanged(): return lax.all_to_all(copies, axes, split_axis=0, concat_axis=0, tiled=True)  23.2 us
    ppermute x12, starting transfers between devices, crossed(): lax.ppermute(x, axis, [(i, i ^ bit) for i in range(lax.axis_size(axis))])  19.1 us
    ppermute x12, waiting for transfers between devices, crossed(): lax.ppermute(x, axis, [(i, i ^ bit) for i in range(lax.axis_size(axis))])  6.53 us
  transfers between devices with their start and end apart: 46, of which 21 were waited for; matrix products, arithmetic and copies ran while one was open for 1% of the time, Pallas kernels for 0%

profile of v1, /device:TPU:1, one launch (start us, length us, event | category | flops | bytes accessed | tf_op | source)
XLA Modules:
  0.0 176.5 jit_solution(14158731154527184076)
XLA Ops:
  1.9 2.4 %prepare.1 = (bf16[288,128]{1,0:T(8,128)(2,1)S(1)}, bf16[8,144,128]{2,1,0:T(8,128)(2,1)}, bf16[144,128]{1,0:T(8,128)(2,1)S(1)}) custom-call(s32[4]{0:T(128)} %pad_add_fusion.at_ref, s32[1,16]{1,0:T(1,128)} %pairs_ref.5, s32[1]{0:T(128)S(6)} %copy.32.counts_ref, s32[32]{0:T(128)} %owner_ref.5, f32[1,128,128]{2,1,0:T(8,128)} %tp_ref.1, f32[1,128]{1,0:T(1,128)} %tl_ref.1, ...), custom_call_target="tpu_custom_call" | custom-call | tf_op jit(solution)/shard_map/prepare/pallas_call | solution.py:327
  4.3 3.3 %collective-permute-start.5 = (bf16[144,128]{1,0:T(8,128)(2,1)S(1)}, bf16[144,128]{1,0:T(8,128)(2,1)S(1)}, u32[]{:S(2)}, u32[]{:S(2)}) collective-permute-start(bf16[144,128]{1,0:T(8,128)(2,1)S(1)} %get-tuple-element.30), channel_id=1, source_target_pairs={{0,192},{64,0},{128,64},{192,128},{1,193},{65,1},{129,65},{193,129... | collective-permute-start | bytes 110600 | tf_op jit(solution)/shard_map/ppermute | solution.py:276
  8.8 8.2 %all-to-all-start = ((bf16[8,144,128]{2,1,0:T(8,128)(2,1)}), bf16[8,144,128]{2,1,0:T(8,128)(2,1)S(1)}, u32[]{:S(2)}, u32[]{:S(2)}) async-start(bf16[8,144,128]{2,1,0:T(8,128)(2,1)} %get-tuple-element.29), calls=%async_computation | async-start | bytes 589824 | tf_op jit(solution)/shard_map/all_to_all | solution.py:271
  17.0 1.5 collective-permute-start.6
  18.5 2.4 %collective-permute-start.13 = (bf16[288,128]{1,0:T(8,128)(2,1)S(1)}, bf16[288,128]{1,0:T(8,128)(2,1)S(1)}, u32[]{:S(2)}, u32[]{:S(2)}) collective-permute-start(bf16[288,128]{1,0:T(8,128)(2,1)S(1)} %get-tuple-element.31), channel_id=1, source_target_pairs={{0,1},{1,0},{2,3},{3,2},{4,5},{5,4},{6,7},{7,6},{8,9},{9,8},{10,11... | collective-permute-start | bytes 221192 | tf_op jit(solution)/shard_map/ppermute | solution.py:280
  21.9 6.9 %collective-permute-done.6.refs_5_ = bf16[4,144,128]{2,1,0:T(8,128)(2,1)S(1)} collective-permute-done((bf16[4,144,128]{2,1,0:T(8,128)(2,1)S(1)}, bf16[4,144,128]{2,1,0:T(8,128)(2,1)S(1)}, u32[]{:S(2)}, u32[]{:S(2)}) %collective-permute-start.6) | collective-permute-done | bytes 147488 | tf_op jit(solution)/shard_map/ppermute | solution.py:276
  29.4 1.3 collective-permute-start.14
  30.7 2.1 %collective-permute-start.11 = (bf16[4,144,128]{2,1,0:T(8,128)(2,1)S(1)}, bf16[4,144,128]{2,1,0:T(8,128)(2,1)S(1)}, u32[]{:S(2)}, u32[]{:S(2)}) collective-permute-start(bf16[4,144,128]{2,1,0:T(8,128)(2,1)S(1)} %collective-permute-done.10.refs_11_), channel_id=1, source_target_pairs={{0,56},{8,0},{16,8},{24,16},{32,24},{40,32},{48,40},{56,48},{1,57}... | collective-permute-start | bytes 442376 | tf_op jit(solution)/shard_map/ppermute | solution.py:276
  32.9 2.1 %collective-permute-start.2 = (bf16[8,144,128]{2,1,0:T(8,128)(2,1)S(1)}, bf16[8,144,128]{2,1,0:T(8,128)(2,1)S(1)}, u32[]{:S(2)}, u32[]{:S(2)}) collective-permute-start(bf16[8,144,128]{2,1,0:T(8,128)(2,1)S(1)} %all-to-all-done.refs_0_), channel_id=1, source_target_pairs={{0,192},{64,0},{128,64},{192,128},{1,193},{65,1},{129,65},{193,129... | collective-permute-start | bytes 884744 | tf_op jit(solution)/shard_map/ppermute | solution.py:276
  35.0 1.3 collective-permute-start.1
  36.7 3.0 %collective-permute-start.15 = (bf16[4,288,128]{2,1,0:T(8,128)(2,1)S(1)}, bf16[4,288,128]{2,1,0:T(8,128)(2,1)S(1)}, u32[]{:S(2)}, u32[]{:S(2)}) collective-permute-start(bf16[4,288,128]{2,1,0:T(8,128)(2,1)S(1)} %pad_maximum_fusion.refs_12_), channel_id=1, source_target_pairs={{0,4},{2,6},{4,0},{6,2},{1,5},{3,7},{5,1},{7,3},{8,12},{10,14},{12... | collective-permute-start | bytes 884744 | tf_op jit(solution)/shard_map/ppermute | solution.py:280
  40.2 2.2 %collective-permute-start.12 = (bf16[4,144,128]{2,1,0:T(8,128)(2,1)S(1)}, bf16[4,144,128]{2,1,0:T(8,128)(2,1)S(1)}, u32[]{:S(2)}, u32[]{:S(2)}) collective-permute-start(bf16[4,144,128]{2,1,0:T(8,128)(2,1)S(1)} %collective-permute-done.11.refs_10_), channel_id=1, source_target_pairs={{0,56},{8,0},{16,8},{24,16},{32,24},{40,32},{48,40},{56,48},{1,57}... | collective-permute-start | bytes 442376 | tf_op jit(solution)/shard_map/ppermute | solution.py:276
  42.5 8.6 %collective-permute-done.refs_1_ = bf16[8,144,128]{2,1,0:T(8,128)(2,1)S(1)} collective-permute-done((bf16[8,144,128]{2,1,0:T(8,128)(2,1)S(1)}, bf16[8,144,128]{2,1,0:T(8,128)(2,1)S(1)}, u32[]{:S(2)}, u32[]{:S(2)}) %collective-permute-start) | collective-permute-done | bytes 294944 | tf_op jit(solution)/shard_map/ppermute | solution.py:276
  51.9 23.5 %attend.2 = (bf16[4,288,128]{2,1,0:T(8,128)(2,1)S(1)}, bf16[4,288,128]{2,1,0:T(8,128)(2,1)S(1)}) custom-call(s32[4]{0:T(128)} %pad_add_fusion.at_ref, s32[1,16]{1,0:T(1,128)} %pairs_ref.5, s32[1]{0:T(128)S(6)} %copy.32.counts_ref, s32[32]{0:T(128)} %owner_ref.5, s32[32]{0:T(128)} %convert_reduce_fusion.named_ref, bf16[8,144,128]{2,1,0:T(8,128)(2,1)} %copy-done, ...), custom_call_target="tpu_custom_call" | custom-call | tf_op jit(solution)/shard_map/attend/pallas_call | solution.py:350
  75.4 3.1 %collective-permute-start.16 = (bf16[4,288,128]{2,1,0:T(8,128)(2,1)S(1)}, bf16[4,288,128]{2,1,0:T(8,128)(2,1)S(1)}, u32[]{:S(2)}, u32[]{:S(2)}) collective-permute-start(bf16[4,288,128]{2,1,0:T(8,128)(2,1)S(1)} %get-tuple-element.33), channel_id=1, source_target_pairs={{0,1},{1,0},{2,3},{3,2},{4,5},{5,4},{6,7},{7,6},{8,9},{9,8},{10,11... | collective-permute-start | bytes 884744 | tf_op jit(solution)/shard_map/ppermute | solution.py:276
  78.5 1.2 collective-permute-done.16.other_ref
  80.4 2.9 %collective-permute-start.18 = (bf16[288,128]{1,0:T(8,128)(2,1)S(1)}, bf16[288,128]{1,0:T(8,128)(2,1)S(1)}, u32[]{:S(2)}, u32[]{:S(2)}) collective-permute-start(bf16[288,128]{1,0:T(8,128)(2,1)S(1)} %get-tuple-element.36), channel_id=1, source_target_pairs={{0,4},{2,6},{4,0},{6,2},{1,5},{3,7},{5,1},{7,3},{8,12},{10,14},{12... | collective-permute-start | bytes 221192 | tf_op jit(solution)/shard_map/ppermute | solution.py:280
  84.1 1.5 dynamic-slice_bitcast_fusion.refs_5_
  86.6 1.6 collective-permute-done.19.refs_3_
  88.2 2.3 %settle.2 = (f32[128,128]{1,0:T(8,128)S(1)}, f32[1,128]{1,0:T(1,128)}, f32[136,128]{1,0:T(8,128)S(1)}, bf16[288,128]{1,0:T(8,128)(2,1)S(1)}, bf16[8,144,128]{2,1,0:T(8,128)(2,1)}, /*index=5*/bf16[144,128]{1,0:T(8,128)(2,1)S(1)}) custom-call(bf16[288,128]{1,0:T(8,128)(2,1)S(1)} %get-tuple-element.34.refs_0_, ...), custom_call_target="tpu_custom_call" | custom-call | tf_op jit(solution)/shard_map/settle/pallas_call | solution.py:382
  90.5 1.5 collective-permute-start.23
  91.9 1.3 collective-permute-done.25
  93.3 1.5 collective-permute-done.24
  95.7 1.1 collective-permute-start.30
  96.8 15.0 %all-to-all-start.1 = ((bf16[8,144,128]{2,1,0:T(8,128)(2,1)}), bf16[8,144,128]{2,1,0:T(8,128)(2,1)S(1)}, u32[]{:S(2)}, u32[]{:S(2)}) async-start(bf16[8,144,128]{2,1,0:T(8,128)(2,1)} %get-tuple-element.38), calls=%async_computation.1 | async-start | bytes 589824 | tf_op jit(solution)/shard_map/all_to_all | solution.py:271
  111.8 3.6 %collective-permute-start.33 = (bf16[288,128]{1,0:T(8,128)(2,1)S(1)}, bf16[288,128]{1,0:T(8,128)(2,1)S(1)}, u32[]{:S(2)}, u32[]{:S(2)}) collective-permute-start(bf16[288,128]{1,0:T(8,128)(2,1)S(1)} %get-tuple-element.40), channel_id=1, source_target_pairs={{0,1},{1,0},{2,3},{3,2},{4,5},{5,4},{6,7},{7,6},{8,9},{9,8},{10,11... | collective-permute-start | bytes 221192 | tf_op jit(solution)/shard_map/ppermute | solution.py:280
  115.4 1.7 collective-permute-start.26
  117.1 1.3 collective-permute-start.31
  118.6 5.3 %collective-permute-done.26.refs_5_ = bf16[4,144,128]{2,1,0:T(8,128)(2,1)S(1)} collective-permute-done((bf16[4,144,128]{2,1,0:T(8,128)(2,1)S(1)}, bf16[4,144,128]{2,1,0:T(8,128)(2,1)S(1)}, u32[]{:S(2)}, u32[]{:S(2)}) %collective-permute-start.26) | collective-permute-done | bytes 147488 | tf_op jit(solution)/shard_map/ppermute | solution.py:276
  124.6 2.0 %collective-permute-start.32 = (bf16[4,144,128]{2,1,0:T(8,128)(2,1)S(1)}, bf16[4,144,128]{2,1,0:T(8,128)(2,1)S(1)}, u32[]{:S(2)}, u32[]{:S(2)}) collective-permute-start(bf16[4,144,128]{2,1,0:T(8,128)(2,1)S(1)} %collective-permute-done.31.refs_10_), channel_id=1, source_target_pairs={{0,56},{8,0},{16,8},{24,16},{32,24},{40,32},{48,40},{56,48},{1,57}... | collective-permute-start | bytes 442376 | tf_op jit(solution)/shard_map/ppermute | solution.py:276
  127.5 1.6 collective-permute-done.27.refs_6_
  129.8 1.2 collective-permute-start.21
  131.8 2.8 %collective-permute-done.28.refs_7_ = bf16[4,144,128]{2,1,0:T(8,128)(2,1)S(1)} collective-permute-done((bf16[4,144,128]{2,1,0:T(8,128)(2,1)S(1)}, bf16[4,144,128]{2,1,0:T(8,128)(2,1)S(1)}, u32[]{:S(2)}, u32[]{:S(2)}) %collective-permute-start.28) | collective-permute-done | bytes 147488 | tf_op jit(solution)/shard_map/ppermute | solution.py:276
  134.6 5.6 %collective-permute-done.29.refs_8_ = bf16[4,144,128]{2,1,0:T(8,128)(2,1)S(1)} collective-permute-done((bf16[4,144,128]{2,1,0:T(8,128)(2,1)S(1)}, bf16[4,144,128]{2,1,0:T(8,128)(2,1)S(1)}, u32[]{:S(2)}, u32[]{:S(2)}) %collective-permute-start.29) | collective-permute-done | bytes 147488 | tf_op jit(solution)/shard_map/ppermute | solution.py:276
  140.2 4.9 %collective-permute-done.20.refs_1_ = bf16[8,144,128]{2,1,0:T(8,128)(2,1)S(1)} collective-permute-done((bf16[8,144,128]{2,1,0:T(8,128)(2,1)S(1)}, bf16[8,144,128]{2,1,0:T(8,128)(2,1)S(1)}, u32[]{:S(2)}, u32[]{:S(2)}) %collective-permute-start.20) | collective-permute-done | bytes 294944 | tf_op jit(solution)/shard_map/ppermute | solution.py:276
  145.1 6.5 %attend.3 = (bf16[4,288,128]{2,1,0:T(8,128)(2,1)S(1)}, bf16[4,288,128]{2,1,0:T(8,128)(2,1)S(1)}) custom-call(s32[4]{0:T(128)} %pad_add_fusion.at_ref, s32[1,16]{1,0:T(1,128)} %pairs_ref.5, s32[1]{0:T(128)S(6)} %copy.32.counts_ref, s32[32]{0:T(128)} %owner_ref.5, s32[32]{0:T(128)} %convert_reduce_fusion.named_ref, bf16[8,144,128]{2,1,0:T(8,128)(2,1)} %copy-done.1, ...), custom_call_target="tpu_custom_call" | custom-call | tf_op jit(solution)/shard_map/attend/pallas_call | solution.py:350
  151.6 2.1 %collective-permute-start.36 = (bf16[4,288,128]{2,1,0:T(8,128)(2,1)S(1)}, bf16[4,288,128]{2,1,0:T(8,128)(2,1)S(1)}, u32[]{:S(2)}, u32[]{:S(2)}) collective-permute-start(bf16[4,288,128]{2,1,0:T(8,128)(2,1)S(1)} %get-tuple-element.42), channel_id=1, source_target_pairs={{0,1},{1,0},{2,3},{3,2},{4,5},{5,4},{6,7},{7,6},{8,9},{9,8},{10,11... | collective-permute-start | bytes 884744 | tf_op jit(solution)/shard_map/ppermute | solution.py:276
  153.6 1.2 collective-permute-done.36.other_ref
  155.8 2.3 %collective-permute-start.38 = (bf16[288,128]{1,0:T(8,128)(2,1)S(1)}, bf16[288,128]{1,0:T(8,128)(2,1)S(1)}, u32[]{:S(2)}, u32[]{:S(2)}) collective-permute-start(bf16[288,128]{1,0:T(8,128)(2,1)S(1)} %get-tuple-element.45), channel_id=1, source_target_pairs={{0,4},{2,6},{4,0},{6,2},{1,5},{3,7},{5,1},{7,3},{8,12},{10,14},{12... | collective-permute-start | bytes 221192 | tf_op jit(solution)/shard_map/ppermute | solution.py:280
  159.2 2.2 %collective-permute-done.38.refs_2_ = bf16[288,128]{1,0:T(8,128)(2,1)S(1)} collective-permute-done((bf16[288,128]{1,0:T(8,128)(2,1)S(1)}, bf16[288,128]{1,0:T(8,128)(2,1)S(1)}, u32[]{:S(2)}, u32[]{:S(2)}) %collective-permute-start.38) | collective-permute-done | bytes 73760 | tf_op jit(solution)/shard_map/ppermute | solution.py:280
  161.4 1.6 collective-permute-done.39.refs_3_
  163.1 1.1 settle.3
  164.2 1.1 collective-permute-start.42
  165.8 1.5 collective-permute-done.42
  167.4 2.7 %collective-permute-done.41 = f32[136,128]{1,0:T(8,128)S(1)} collective-permute-done((f32[136,128]{1,0:T(8,128)S(1)}, f32[136,128]{1,0:T(8,128)S(1)}, u32[]{:S(2)}, u32[]{:S(2)}) %collective-permute-start.41) | collective-permute-done | bytes 69664 | tf_op jit(solution)/shard_map/ppermute | solution.py:276
  170.5 3.2 %collective-permute-start.43 = (f32[4,136,128]{2,1,0:T(8,128)S(1)}, f32[4,136,128]{2,1,0:T(8,128)S(1)}, u32[]{:S(2)}, u32[]{:S(2)}) collective-permute-start(f32[4,136,128]{2,1,0:T(8,128)S(1)} %pad_maximum_fusion.2.refs_0_), channel_id=1, source_target_pairs={{0,1},{1,0},{2,3},{3,2},{4,5},{5,4},{6,7},{7,6},{8,9},{9,8},{10,11... | collective-permute-start | bytes 835592 | tf_op jit(solution)/shard_map/ppermute | solution.py:276
  173.8 1.2 collective-permute-done.43.refs_1_
  175.0 1.5 finish.1
  (102 shorter events, 14.6 us)
Async XLA Ops:
  4.3 12.6 %collective-permute-start.5 = (bf16[144,128]{1,0:T(8,128)(2,1)S(1)}, bf16[144,128]{1,0:T(8,128)(2,1)S(1)}, u32[]{:S(2)}, u32[]{:S(2)}) collective-permute-start(bf16[144,128]{1,0:T(8,128)(2,1)S(1)} %get-tuple-element.30), channel_id=1, source_target_pairs={{0,192},{64,0},{128,64},{192,128},{1,193},{65,1},{129,65},{193,129... | collective-permute-start | bytes 110600 | tf_op jit(solution)/shard_map/ppermute | solution.py:276
  7.6 9.3 %collective-permute-start.4 = (bf16[144,128]{1,0:T(8,128)(2,1)S(1)}, bf16[144,128]{1,0:T(8,128)(2,1)S(1)}, u32[]{:S(2)}, u32[]{:S(2)}) collective-permute-start(bf16[144,128]{1,0:T(8,128)(2,1)S(1)} %get-tuple-element.30), channel_id=1, source_target_pairs={{0,128},{64,192},{128,0},{192,64},{1,129},{65,193},{129,1},{193,65... | collective-permute-start | bytes 110600 | tf_op jit(solution)/shard_map/ppermute | solution.py:276
  8.2 8.8 %collective-permute-start.3 = (bf16[144,128]{1,0:T(8,128)(2,1)S(1)}, bf16[144,128]{1,0:T(8,128)(2,1)S(1)}, u32[]{:S(2)}, u32[]{:S(2)}) collective-permute-start(bf16[144,128]{1,0:T(8,128)(2,1)S(1)} %get-tuple-element.30), channel_id=1, source_target_pairs={{0,64},{64,128},{128,192},{192,0},{1,65},{65,129},{129,193},{193,1... | collective-permute-start | bytes 110600 | tf_op jit(solution)/shard_map/ppermute | solution.py:276
  8.8 24.1 %all-to-all-start = ((bf16[8,144,128]{2,1,0:T(8,128)(2,1)}), bf16[8,144,128]{2,1,0:T(8,128)(2,1)S(1)}, u32[]{:S(2)}, u32[]{:S(2)}) async-start(bf16[8,144,128]{2,1,0:T(8,128)(2,1)} %get-tuple-element.29), calls=%async_computation | async-start | bytes 589824 | tf_op jit(solution)/shard_map/all_to_all | solution.py:271
  17.0 11.8 %collective-permute-start.6 = (bf16[4,144,128]{2,1,0:T(8,128)(2,1)S(1)}, bf16[4,144,128]{2,1,0:T(8,128)(2,1)S(1)}, u32[]{:S(2)}, u32[]{:S(2)}) collective-permute-start(bf16[4,144,128]{2,1,0:T(8,128)(2,1)S(1)} %pad_maximum_fusion.3.refs_4_), channel_id=1, source_target_pairs={{0,8},{8,16},{16,24},{24,32},{32,40},{40,48},{48,56},{56,0},{1,9},... | collective-permute-start | bytes 442376 | tf_op jit(solution)/shard_map/ppermute | solution.py:276
  18.5 10.3 %collective-permute-start.13 = (bf16[288,128]{1,0:T(8,128)(2,1)S(1)}, bf16[288,128]{1,0:T(8,128)(2,1)S(1)}, u32[]{:S(2)}, u32[]{:S(2)}) collective-permute-start(bf16[288,128]{1,0:T(8,128)(2,1)S(1)} %get-tuple-element.31), channel_id=1, source_target_pairs={{0,1},{1,0},{2,3},{3,2},{4,5},{5,4},{6,7},{7,6},{8,9},{9,8},{10,11... | collective-permute-start | bytes 221192 | tf_op jit(solution)/shard_map/ppermute | solution.py:280
  20.9 9.9 %collective-permute-start.10 = (bf16[4,144,128]{2,1,0:T(8,128)(2,1)S(1)}, bf16[4,144,128]{2,1,0:T(8,128)(2,1)S(1)}, u32[]{:S(2)}, u32[]{:S(2)}) collective-permute-start(bf16[4,144,128]{2,1,0:T(8,128)(2,1)S(1)} %pad_maximum_fusion.3.refs_4_), channel_id=1, source_target_pairs={{0,56},{8,0},{16,8},{24,16},{32,24},{40,32},{48,40},{56,48},{1,57}... | collective-permute-start | bytes 442376 | tf_op jit(solution)/shard_map/ppermute | solution.py:276
  28.8 6.2 %collective-permute-start.7 = (bf16[4,144,128]{2,1,0:T(8,128)(2,1)S(1)}, bf16[4,144,128]{2,1,0:T(8,128)(2,1)S(1)}, u32[]{:S(2)}, u32[]{:S(2)}) collective-permute-start(bf16[4,144,128]{2,1,0:T(8,128)(2,1)S(1)} %collective-permute-done.6.refs_5_), channel_id=1, source_target_pairs={{0,8},{8,16},{16,24},{24,32},{32,40},{40,48},{48,56},{56,0},{1,9},... | collective-permute-start | bytes 442376 | tf_op jit(solution)/shard_map/ppermute | solution.py:276
  29.4 6.9 %collective-permute-start.14 = (bf16[2,288,128]{2,1,0:T(8,128)(2,1)S(1)}, bf16[2,288,128]{2,1,0:T(8,128)(2,1)S(1)}, u32[]{:S(2)}, u32[]{:S(2)}) collective-permute-start(bf16[2,288,128]{2,1,0:T(8,128)(2,1)S(1)} %pad_maximum_fusion.4), channel_id=1, source_target_pairs={{0,2},{2,0},{4,6},{6,4},{1,3},{3,1},{5,7},{7,5},{8,10},{10,8},{12,... | collective-permute-start | bytes 442376 | tf_op jit(solution)/shard_map/ppermute | solution.py:280
  30.7 6.0 %collective-permute-start.11 = (bf16[4,144,128]{2,1,0:T(8,128)(2,1)S(1)}, bf16[4,144,128]{2,1,0:T(8,128)(2,1)S(1)}, u32[]{:S(2)}, u32[]{:S(2)}) collective-permute-start(bf16[4,144,128]{2,1,0:T(8,128)(2,1)S(1)} %collective-permute-done.10.refs_11_), channel_id=1, source_target_pairs={{0,56},{8,0},{16,8},{24,16},{32,24},{40,32},{48,40},{56,48},{1,57}... | collective-permute-start | bytes 442376 | tf_op jit(solution)/shard_map/ppermute | solution.py:276
  32.9 9.5 %collective-permute-start.2 = (bf16[8,144,128]{2,1,0:T(8,128)(2,1)S(1)}, bf16[8,144,128]{2,1,0:T(8,128)(2,1)S(1)}, u32[]{:S(2)}, u32[]{:S(2)}) collective-permute-start(bf16[8,144,128]{2,1,0:T(8,128)(2,1)S(1)} %all-to-all-done.refs_0_), channel_id=1, source_target_pairs={{0,192},{64,0},{128,64},{192,128},{1,193},{65,1},{129,65},{193,129... | collective-permute-start | bytes 884744 | tf_op jit(solution)/shard_map/ppermute | solution.py:276
  35.0 5.2 %collective-permute-start.8 = (bf16[4,144,128]{2,1,0:T(8,128)(2,1)S(1)}, bf16[4,144,128]{2,1,0:T(8,128)(2,1)S(1)}, u32[]{:S(2)}, u32[]{:S(2)}) collective-permute-start(bf16[4,144,128]{2,1,0:T(8,128)(2,1)S(1)} %collective-permute-done.7.refs_6_), channel_id=1, source_target_pairs={{0,8},{8,16},{16,24},{24,32},{32,40},{40,48},{48,56},{56,0},{1,9},... | collective-permute-start | bytes 442376 | tf_op jit(solution)/shard_map/ppermute | solution.py:276
  35.0 7.5 %collective-permute-start.1 = (bf16[8,144,128]{2,1,0:T(8,128)(2,1)S(1)}, bf16[8,144,128]{2,1,0:T(8,128)(2,1)S(1)}, u32[]{:S(2)}, u32[]{:S(2)}) collective-permute-start(bf16[8,144,128]{2,1,0:T(8,128)(2,1)S(1)} %all-to-all-done.refs_0_), channel_id=1, source_target_pairs={{0,128},{64,192},{128,0},{192,64},{1,129},{65,193},{129,1},{193,65... | collective-permute-start | bytes 884744 | tf_op jit(solution)/shard_map/ppermute | solution.py:276
  36.3 14.8 %collective-permute-start = (bf16[8,144,128]{2,1,0:T(8,128)(2,1)S(1)}, bf16[8,144,128]{2,1,0:T(8,128)(2,1)S(1)}, u32[]{:S(2)}, u32[]{:S(2)}) collective-permute-start(bf16[8,144,128]{2,1,0:T(8,128)(2,1)S(1)} %all-to-all-done.refs_0_), channel_id=1, source_target_pairs={{0,64},{64,128},{128,192},{192,0},{1,65},{65,129},{129,193},{193,1... | collective-permute-start | bytes 884744 | tf_op jit(solution)/shard_map/ppermute | solution.py:276
  36.7 15.1 %collective-permute-start.15 = (bf16[4,288,128]{2,1,0:T(8,128)(2,1)S(1)}, bf16[4,288,128]{2,1,0:T(8,128)(2,1)S(1)}, u32[]{:S(2)}, u32[]{:S(2)}) collective-permute-start(bf16[4,288,128]{2,1,0:T(8,128)(2,1)S(1)} %pad_maximum_fusion.refs_12_), channel_id=1, source_target_pairs={{0,4},{2,6},{4,0},{6,2},{1,5},{3,7},{5,1},{7,3},{8,12},{10,14},{12... | collective-permute-start | bytes 884744 | tf_op jit(solution)/shard_map/ppermute | solution.py:280
  40.2 11.7 %collective-permute-start.12 = (bf16[4,144,128]{2,1,0:T(8,128)(2,1)S(1)}, bf16[4,144,128]{2,1,0:T(8,128)(2,1)S(1)}, u32[]{:S(2)}, u32[]{:S(2)}) collective-permute-start(bf16[4,144,128]{2,1,0:T(8,128)(2,1)S(1)} %collective-permute-done.11.refs_10_), channel_id=1, source_target_pairs={{0,56},{8,0},{16,8},{24,16},{32,24},{40,32},{48,40},{56,48},{1,57}... | collective-permute-start | bytes 442376 | tf_op jit(solution)/shard_map/ppermute | solution.py:276
  42.4 9.5 %collective-permute-start.9 = (bf16[4,144,128]{2,1,0:T(8,128)(2,1)S(1)}, bf16[4,144,128]{2,1,0:T(8,128)(2,1)S(1)}, u32[]{:S(2)}, u32[]{:S(2)}) collective-permute-start(bf16[4,144,128]{2,1,0:T(8,128)(2,1)S(1)} %collective-permute-done.8.refs_7_), channel_id=1, source_target_pairs={{0,8},{8,16},{16,24},{24,32},{32,40},{40,48},{48,56},{56,0},{1,9},... | collective-permute-start | bytes 442376 | tf_op jit(solution)/shard_map/ppermute | solution.py:276
  75.4 4.3 %collective-permute-start.16 = (bf16[4,288,128]{2,1,0:T(8,128)(2,1)S(1)}, bf16[4,288,128]{2,1,0:T(8,128)(2,1)S(1)}, u32[]{:S(2)}, u32[]{:S(2)}) collective-permute-start(bf16[4,288,128]{2,1,0:T(8,128)(2,1)S(1)} %get-tuple-element.33), channel_id=1, source_target_pairs={{0,1},{1,0},{2,3},{3,2},{4,5},{5,4},{6,7},{7,6},{8,9},{9,8},{10,11... | collective-permute-start | bytes 884744 | tf_op jit(solution)/shard_map/ppermute | solution.py:276
  80.1 5.4 %collective-permute-start.17 = (bf16[288,128]{1,0:T(8,128)(2,1)S(1)}, bf16[288,128]{1,0:T(8,128)(2,1)S(1)}, u32[]{:S(2)}, u32[]{:S(2)}) collective-permute-start(bf16[288,128]{1,0:T(8,128)(2,1)S(1)} %get-tuple-element.35), channel_id=1, source_target_pairs={{0,2},{2,0},{4,6},{6,4},{1,3},{3,1},{5,7},{7,5},{8,10},{10,8},{12,... | collective-permute-start | bytes 221192 | tf_op jit(solution)/shard_map/ppermute | solution.py:280
  80.4 6.2 %collective-permute-start.18 = (bf16[288,128]{1,0:T(8,128)(2,1)S(1)}, bf16[288,128]{1,0:T(8,128)(2,1)S(1)}, u32[]{:S(2)}, u32[]{:S(2)}) collective-permute-start(bf16[288,128]{1,0:T(8,128)(2,1)S(1)} %get-tuple-element.36), channel_id=1, source_target_pairs={{0,4},{2,6},{4,0},{6,2},{1,5},{3,7},{5,1},{7,3},{8,12},{10,14},{12... | collective-permute-start | bytes 221192 | tf_op jit(solution)/shard_map/ppermute | solution.py:280
  83.3 4.9 %collective-permute-start.19 = (bf16[288,128]{1,0:T(8,128)(2,1)S(1)}, bf16[288,128]{1,0:T(8,128)(2,1)S(1)}, u32[]{:S(2)}, u32[]{:S(2)}) collective-permute-start(bf16[288,128]{1,0:T(8,128)(2,1)S(1)} %get-tuple-element.37), channel_id=1, source_target_pairs={{0,6},{2,4},{4,2},{6,0},{1,7},{3,5},{5,3},{7,1},{8,14},{10,12},{12... | collective-permute-start | bytes 221192 | tf_op jit(solution)/shard_map/ppermute | solution.py:280
  90.5 2.8 %collective-permute-start.25 = (bf16[144,128]{1,0:T(8,128)(2,1)S(1)}, bf16[144,128]{1,0:T(8,128)(2,1)S(1)}, u32[]{:S(2)}, u32[]{:S(2)}) collective-permute-start(bf16[144,128]{1,0:T(8,128)(2,1)S(1)} %get-tuple-element.39), channel_id=1, source_target_pairs={{0,192},{64,0},{128,64},{192,128},{1,193},{65,1},{129,65},{193,129... | collective-permute-start | bytes 110600 | tf_op jit(solution)/shard_map/ppermute | solution.py:276
  90.5 4.3 %collective-permute-start.24 = (bf16[144,128]{1,0:T(8,128)(2,1)S(1)}, bf16[144,128]{1,0:T(8,128)(2,1)S(1)}, u32[]{:S(2)}, u32[]{:S(2)}) collective-permute-start(bf16[144,128]{1,0:T(8,128)(2,1)S(1)} %get-tuple-element.39), channel_id=1, source_target_pairs={{0,128},{64,192},{128,0},{192,64},{1,129},{65,193},{129,1},{193,65... | collective-permute-start | bytes 110600 | tf_op jit(solution)/shard_map/ppermute | solution.py:276
  90.5 5.2 %collective-permute-start.23 = (bf16[144,128]{1,0:T(8,128)(2,1)S(1)}, bf16[144,128]{1,0:T(8,128)(2,1)S(1)}, u32[]{:S(2)}, u32[]{:S(2)}) collective-permute-start(bf16[144,128]{1,0:T(8,128)(2,1)S(1)} %get-tuple-element.39), channel_id=1, source_target_pairs={{0,64},{64,128},{128,192},{192,0},{1,65},{65,129},{129,193},{193,1... | collective-permute-start | bytes 110600 | tf_op jit(solution)/shard_map/ppermute | solution.py:276
  95.7 19.7 %copy-start.5 = (bf16[4,144,128]{2,1,0:T(8,128)(2,1)}, bf16[4,144,128]{2,1,0:T(8,128)(2,1)S(1)}, u32[]{:S(2)}) copy-start(bf16[4,144,128]{2,1,0:T(8,128)(2,1)S(1)} %pad_maximum_fusion.5.refs_4_) | copy-start | bytes 442372
  95.7 21.4 %collective-permute-start.30 = (bf16[4,144,128]{2,1,0:T(8,128)(2,1)S(1)}, bf16[4,144,128]{2,1,0:T(8,128)(2,1)S(1)}, u32[]{:S(2)}, u32[]{:S(2)}) collective-permute-start(bf16[4,144,128]{2,1,0:T(8,128)(2,1)S(1)} %pad_maximum_fusion.5.refs_4_), channel_id=1, source_target_pairs={{0,56},{8,0},{16,8},{24,16},{32,24},{40,32},{48,40},{56,48},{1,57}... | collective-permute-start | bytes 442376 | tf_op jit(solution)/shard_map/ppermute | solution.py:276
  96.8 32.3 %all-to-all-start.1 = ((bf16[8,144,128]{2,1,0:T(8,128)(2,1)}), bf16[8,144,128]{2,1,0:T(8,128)(2,1)S(1)}, u32[]{:S(2)}, u32[]{:S(2)}) async-start(bf16[8,144,128]{2,1,0:T(8,128)(2,1)} %get-tuple-element.38), calls=%async_computation.1 | async-start | bytes 589824 | tf_op jit(solution)/shard_map/all_to_all | solution.py:271
  111.8 6.6 %collective-permute-start.33 = (bf16[288,128]{1,0:T(8,128)(2,1)S(1)}, bf16[288,128]{1,0:T(8,128)(2,1)S(1)}, u32[]{:S(2)}, u32[]{:S(2)}) collective-permute-start(bf16[288,128]{1,0:T(8,128)(2,1)S(1)} %get-tuple-element.40), channel_id=1, source_target_pairs={{0,1},{1,0},{2,3},{3,2},{4,5},{5,4},{6,7},{7,6},{8,9},{9,8},{10,11... | collective-permute-start | bytes 221192 | tf_op jit(solution)/shard_map/ppermute | solution.py:280
  115.4 8.5 %collective-permute-start.26 = (bf16[4,144,128]{2,1,0:T(8,128)(2,1)S(1)}, bf16[4,144,128]{2,1,0:T(8,128)(2,1)S(1)}, u32[]{:S(2)}, u32[]{:S(2)}) collective-permute-start(bf16[4,144,128]{2,1,0:T(8,128)(2,1)S(1)} %pad_maximum_fusion.5.refs_4_), channel_id=1, source_target_pairs={{0,8},{8,16},{16,24},{24,32},{32,40},{40,48},{48,56},{56,0},{1,9},... | collective-permute-start | bytes 442376 | tf_op jit(solution)/shard_map/ppermute | solution.py:276
  117.1 7.4 %collective-permute-start.31 = (bf16[4,144,128]{2,1,0:T(8,128)(2,1)S(1)}, bf16[4,144,128]{2,1,0:T(8,128)(2,1)S(1)}, u32[]{:S(2)}, u32[]{:S(2)}) collective-permute-start(bf16[4,144,128]{2,1,0:T(8,128)(2,1)S(1)} %collective-permute-done.30.refs_11_), channel_id=1, source_target_pairs={{0,56},{8,0},{16,8},{24,16},{32,24},{40,32},{48,40},{56,48},{1,57}... | collective-permute-start | bytes 442376 | tf_op jit(solution)/shard_map/ppermute | solution.py:276
  118.5 8.1 %collective-permute-start.34 = (bf16[2,288,128]{2,1,0:T(8,128)(2,1)S(1)}, bf16[2,288,128]{2,1,0:T(8,128)(2,1)S(1)}, u32[]{:S(2)}, u32[]{:S(2)}) collective-permute-start(bf16[2,288,128]{2,1,0:T(8,128)(2,1)S(1)} %pad_maximum_fusion.6), channel_id=1, source_target_pairs={{0,2},{2,0},{4,6},{6,4},{1,3},{3,1},{5,7},{7,5},{8,10},{10,8},{12,... | collective-permute-start | bytes 442376 | tf_op jit(solution)/shard_map/ppermute | solution.py:280
  123.9 5.2 %collective-permute-start.27 = (bf16[4,144,128]{2,1,0:T(8,128)(2,1)S(1)}, bf16[4,144,128]{2,1,0:T(8,128)(2,1)S(1)}, u32[]{:S(2)}, u32[]{:S(2)}) collective-permute-start(bf16[4,144,128]{2,1,0:T(8,128)(2,1)S(1)} %collective-permute-done.26.refs_5_), channel_id=1, source_target_pairs={{0,8},{8,16},{16,24},{24,32},{32,40},{40,48},{48,56},{56,0},{1,9},... | collective-permute-start | bytes 442376 | tf_op jit(solution)/shard_map/ppermute | solution.py:276
  124.6 6.4 %collective-permute-start.32 = (bf16[4,144,128]{2,1,0:T(8,128)(2,1)S(1)}, bf16[4,144,128]{2,1,0:T(8,128)(2,1)S(1)}, u32[]{:S(2)}, u32[]{:S(2)}) collective-permute-start(bf16[4,144,128]{2,1,0:T(8,128)(2,1)S(1)} %collective-permute-done.31.refs_10_), channel_id=1, source_target_pairs={{0,56},{8,0},{16,8},{24,16},{32,24},{40,32},{48,40},{56,48},{1,57}... | collective-permute-start | bytes 442376 | tf_op jit(solution)/shard_map/ppermute | solution.py:276
  126.6 18.4 %copy-start.3 = (bf16[4,288,128]{2,1,0:T(8,128)(2,1)}, bf16[4,288,128]{2,1,0:T(8,128)(2,1)S(1)}, u32[]{:S(2)}) copy-start(bf16[4,288,128]{2,1,0:T(8,128)(2,1)S(1)} %pad_maximum_fusion.1.refs_12_) | copy-start | bytes 884740
  126.6 8.0 %collective-permute-start.35 = (bf16[4,288,128]{2,1,0:T(8,128)(2,1)S(1)}, bf16[4,288,128]{2,1,0:T(8,128)(2,1)S(1)}, u32[]{:S(2)}, u32[]{:S(2)}) collective-permute-start(bf16[4,288,128]{2,1,0:T(8,128)(2,1)S(1)} %pad_maximum_fusion.1.refs_12_), channel_id=1, source_target_pairs={{0,4},{2,6},{4,0},{6,2},{1,5},{3,7},{5,1},{7,3},{8,12},{10,14},{12... | collective-permute-start | bytes 884744 | tf_op jit(solution)/shard_map/ppermute | solution.py:280
  129.1 5.5 %collective-permute-start.28 = (bf16[4,144,128]{2,1,0:T(8,128)(2,1)S(1)}, bf16[4,144,128]{2,1,0:T(8,128)(2,1)S(1)}, u32[]{:S(2)}, u32[]{:S(2)}) collective-permute-start(bf16[4,144,128]{2,1,0:T(8,128)(2,1)S(1)} %collective-permute-done.27.refs_6_), channel_id=1, source_target_pairs={{0,8},{8,16},{16,24},{24,32},{32,40},{40,48},{48,56},{56,0},{1,9},... | collective-permute-start | bytes 442376 | tf_op jit(solution)/shard_map/ppermute | solution.py:276
  129.1 11.1 %collective-permute-start.22 = (bf16[8,144,128]{2,1,0:T(8,128)(2,1)S(1)}, bf16[8,144,128]{2,1,0:T(8,128)(2,1)S(1)}, u32[]{:S(2)}, u32[]{:S(2)}) collective-permute-start(bf16[8,144,128]{2,1,0:T(8,128)(2,1)S(1)} %all-to-all-done.1.refs_0_), channel_id=1, source_target_pairs={{0,192},{64,0},{128,64},{192,128},{1,193},{65,1},{129,65},{193,129... | collective-permute-start | bytes 884744 | tf_op jit(solution)/shard_map/ppermute | solution.py:276
  129.8 10.4 %collective-permute-start.21 = (bf16[8,144,128]{2,1,0:T(8,128)(2,1)S(1)}, bf16[8,144,128]{2,1,0:T(8,128)(2,1)S(1)}, u32[]{:S(2)}, u32[]{:S(2)}) collective-permute-start(bf16[8,144,128]{2,1,0:T(8,128)(2,1)S(1)} %all-to-all-done.1.refs_0_), channel_id=1, source_target_pairs={{0,128},{64,192},{128,0},{192,64},{1,129},{65,193},{129,1},{193,65... | collective-permute-start | bytes 884744 | tf_op jit(solution)/shard_map/ppermute | solution.py:276
  131.0 14.1 %collective-permute-start.20 = (bf16[8,144,128]{2,1,0:T(8,128)(2,1)S(1)}, bf16[8,144,128]{2,1,0:T(8,128)(2,1)S(1)}, u32[]{:S(2)}, u32[]{:S(2)}) collective-permute-start(bf16[8,144,128]{2,1,0:T(8,128)(2,1)S(1)} %all-to-all-done.1.refs_0_), channel_id=1, source_target_pairs={{0,64},{64,128},{128,192},{192,0},{1,65},{65,129},{129,193},{193,1... | collective-permute-start | bytes 884744 | tf_op jit(solution)/shard_map/ppermute | solution.py:276
  134.6 5.6 %collective-permute-start.29 = (bf16[4,144,128]{2,1,0:T(8,128)(2,1)S(1)}, bf16[4,144,128]{2,1,0:T(8,128)(2,1)S(1)}, u32[]{:S(2)}, u32[]{:S(2)}) collective-permute-start(bf16[4,144,128]{2,1,0:T(8,128)(2,1)S(1)} %collective-permute-done.28.refs_7_), channel_id=1, source_target_pairs={{0,8},{8,16},{16,24},{24,32},{32,40},{40,48},{48,56},{56,0},{1,9},... | collective-permute-start | bytes 442376 | tf_op jit(solution)/shard_map/ppermute | solution.py:276
  151.6 3.3 %collective-permute-start.36 = (bf16[4,288,128]{2,1,0:T(8,128)(2,1)S(1)}, bf16[4,288,128]{2,1,0:T(8,128)(2,1)S(1)}, u32[]{:S(2)}, u32[]{:S(2)}) collective-permute-start(bf16[4,288,128]{2,1,0:T(8,128)(2,1)S(1)} %get-tuple-element.42), channel_id=1, source_target_pairs={{0,1},{1,0},{2,3},{3,2},{4,5},{5,4},{6,7},{7,6},{8,9},{9,8},{10,11... | collective-permute-start | bytes 884744 | tf_op jit(solution)/shard_map/ppermute | solution.py:276
  155.2 3.9 %collective-permute-start.37 = (bf16[288,128]{1,0:T(8,128)(2,1)S(1)}, bf16[288,128]{1,0:T(8,128)(2,1)S(1)}, u32[]{:S(2)}, u32[]{:S(2)}) collective-permute-start(bf16[288,128]{1,0:T(8,128)(2,1)S(1)} %get-tuple-element.44), channel_id=1, source_target_pairs={{0,2},{2,0},{4,6},{6,4},{1,3},{3,1},{5,7},{7,5},{8,10},{10,8},{12,... | collective-permute-start | bytes 221192 | tf_op jit(solution)/shard_map/ppermute | solution.py:280
  155.8 5.6 %collective-permute-start.38 = (bf16[288,128]{1,0:T(8,128)(2,1)S(1)}, bf16[288,128]{1,0:T(8,128)(2,1)S(1)}, u32[]{:S(2)}, u32[]{:S(2)}) collective-permute-start(bf16[288,128]{1,0:T(8,128)(2,1)S(1)} %get-tuple-element.45), channel_id=1, source_target_pairs={{0,4},{2,6},{4,0},{6,2},{1,5},{3,7},{5,1},{7,3},{8,12},{10,14},{12... | collective-permute-start | bytes 221192 | tf_op jit(solution)/shard_map/ppermute | solution.py:280
  158.2 4.9 %collective-permute-start.39 = (bf16[288,128]{1,0:T(8,128)(2,1)S(1)}, bf16[288,128]{1,0:T(8,128)(2,1)S(1)}, u32[]{:S(2)}, u32[]{:S(2)}) collective-permute-start(bf16[288,128]{1,0:T(8,128)(2,1)S(1)} %get-tuple-element.46), channel_id=1, source_target_pairs={{0,6},{2,4},{4,2},{6,0},{1,7},{3,5},{5,3},{7,1},{8,14},{10,12},{12... | collective-permute-start | bytes 221192 | tf_op jit(solution)/shard_map/ppermute | solution.py:280
  164.2 3.2 %collective-permute-start.42 = (f32[136,128]{1,0:T(8,128)S(1)}, f32[136,128]{1,0:T(8,128)S(1)}, u32[]{:S(2)}, u32[]{:S(2)}) collective-permute-start(f32[136,128]{1,0:T(8,128)S(1)} %get-tuple-element.49), channel_id=1, source_target_pairs={{0,6},{2,0},{4,2},{6,4},{1,7},{3,1},{5,3},{7,5},{8,14},{10,8},{12,... | collective-permute-start | bytes 208904 | tf_op jit(solution)/shard_map/ppermute | solution.py:276
  165.3 4.8 %collective-permute-start.41 = (f32[136,128]{1,0:T(8,128)S(1)}, f32[136,128]{1,0:T(8,128)S(1)}, u32[]{:S(2)}, u32[]{:S(2)}) collective-permute-start(f32[136,128]{1,0:T(8,128)S(1)} %get-tuple-element.49), channel_id=1, source_target_pairs={{0,4},{2,6},{4,0},{6,2},{1,5},{3,7},{5,1},{7,3},{8,12},{10,14},{12... | collective-permute-start | bytes 208904 | tf_op jit(solution)/shard_map/ppermute | solution.py:276
  165.3 5.2 %collective-permute-start.40 = (f32[136,128]{1,0:T(8,128)S(1)}, f32[136,128]{1,0:T(8,128)S(1)}, u32[]{:S(2)}, u32[]{:S(2)}) collective-permute-start(f32[136,128]{1,0:T(8,128)S(1)} %get-tuple-element.49), channel_id=1, source_target_pairs={{0,2},{2,4},{4,6},{6,0},{1,3},{3,5},{5,7},{7,1},{8,10},{10,12},{12... | collective-permute-start | bytes 208904 | tf_op jit(solution)/shard_map/ppermute | solution.py:276
  170.5 4.4 %collective-permute-start.43 = (f32[4,136,128]{2,1,0:T(8,128)S(1)}, f32[4,136,128]{2,1,0:T(8,128)S(1)}, u32[]{:S(2)}, u32[]{:S(2)}) collective-permute-start(f32[4,136,128]{2,1,0:T(8,128)S(1)} %pad_maximum_fusion.2.refs_0_), channel_id=1, source_target_pairs={{0,1},{1,0},{2,3},{3,2},{4,5},{5,4},{6,7},{7,6},{8,9},{9,8},{10,11... | collective-permute-start | bytes 835592 | tf_op jit(solution)/shard_map/ppermute | solution.py:276
  (14 other events, 120.2 us)

commit v2 on v1

--- a/solution.py
+++ b/solution.py
@@ -28,10 +28,6 @@
 LANES = (((1,), (1,)), ((), ()))
 
 
-def as_row(column):
-    return jnp.broadcast_to(column, (SHARD, WIDTH)).T[:16]
-
-
 def in_three(rows):
     hi = rows.astype(BF16)
     rest = rows - hi.astype(F32)
@@ -49,7 +45,13 @@
 
 def square_row(rounded):
     wide = rounded.astype(F32)
-    return as_row(jnp.sum(wide * wide, axis=1, keepdims=True))
+    square = wide * wide
+    hi = square.astype(BF16)
+    mid = (square - hi.astype(F32)).astype(BF16)
+    ones = jnp.ones((16, WIDTH), BF16)
+    return lax.dot_general(ones, hi, LANES, preferred_element_type=F32) + lax.dot_general(
+        ones, mid, LANES, preferred_element_type=F32
+    )
 
 
 def write_side(msg_ref, copies_ref, source_ref, side, points, level_row, meta=None):
@@ -287,12 +289,17 @@
 
 
 def from_helpers_late(msg):
-    own = jnp.stack([shifted(msg, "y", k) if k else msg for k in range(YS)])
+    parts = [msg]
+    for k in range(1, YS):
+        parts.append(shifted(msg, "y", k))
+    own = jnp.stack(parts)
     return own, shifted(own, "c", 1)
 
 
 def from_blocks(copies, source):
-    sides = [source] + [shifted(source, "x", k) for k in range(1, XS)]
+    sides = [source]
+    for k in range(1, XS):
+        sides.append(shifted(source, "x", k))
     near = exchanged(copies, "z")
     ring = [None] * ZS
     ring[0] = ahead = back = jnp.stack(sides)
@@ -321,8 +328,8 @@
     source_shape = pltpu.VMEM((SIDE, WIDTH), BF16)
     half_shape = pltpu.VMEM((YS, MSG, WIDTH), BF16)
     final_shape = pltpu.VMEM((SHARD + 8, WIDTH), F32)
-    own_points = pl.BlockSpec((1, SHARD, WIDTH), lambda i, at: (0, at[2] * CS + at[3], 0))
-    own_level = pl.BlockSpec((1, SHARD), lambda i, at: (0, at[2] * CS + at[3]))
+    own_points = pl.BlockSpec((1, SHARD, WIDTH), lambda i, at: (0, at[0], 0))
+    own_level = pl.BlockSpec((1, SHARD), lambda i, at: (0, at[0]))
     whole = lambda *shape: pl.BlockSpec(shape, lambda i, at: (0,) * len(shape))
     msg, copies, source = pl.pallas_call(
         prepare_kernel,
@@ -334,7 +341,7 @@
             out_specs=(whole(*msg_shape.shape), whole(*copies_shape.shape), whole(*source_shape.shape)),
         ),
         name="prepare",
-    )(at, pairs, counts, owner, target_points, target_potential, source_points, source_potential)
+    )(helper[None], pairs, counts, owner, target_points, target_potential, source_points, source_potential)
     tp = target_points[0]
     sp = lax.dynamic_slice_in_dim(source_points[0], helper * SHARD, SHARD, 0)
     points_shape = jax.ShapeDtypeStruct((SHARD, WIDTH), F32)
@@ -376,7 +383,9 @@
             scratch_shapes=[pltpu.VMEM((WIDTH, SHARD), F32)],
             name="merge",
         )(*near_core(own, other))
-        got = [crossed(part, "y", k) if k else part for k, part in enumerate(merged)]
+        got = [merged[0]]
+        for k in range(1, YS):
+            got.append(crossed(merged[k], "y", k))
         last = step == ITERS - 1
         messages = () if last else (msg_shape, copies_shape, source_shape)
         tp, tl, sp, *rest = pl.pallas_call(
@@ -388,13 +397,14 @@
             name="settle",
         )(*near_core(*got), *((tp, sp) if step == 0 else near_core(tp, sp)))
         msg, copies, source = rest or (None,) * 3
+    pieces = near_core(*from_helpers_late(sp))
     new_source_points, new_source_potential = pl.pallas_call(
         finish_kernel,
         out_shape=(jax.ShapeDtypeStruct(source_points.shape, F32), jax.ShapeDtypeStruct((helpers, SHARD), F32)),
         in_specs=[smem, vmem, vmem],
         out_specs=(vmem, vmem),
         name="finish",
-    )(at, *near_core(*from_helpers_late(sp)))
+    )(at, *pieces)
     return new_source_points, new_source_potential.reshape(source_potential.shape), tp[None], tl
 
 

time: 177 us -> 175 us (0.989)
  transfers between devices with their start and end apart: 46 -> 46, of which waited for: 21 -> 21; matrix products, arithmetic and copies ran while one was open for 1% -> 2% of each run, Pallas kernels for 0% -> 0%
where the time goes in v2:
time: 175 us
  starting transfers between devices  78.3 us (45%)
  waiting for transfers between devices  54.1 us (31%)
  Pallas kernels  37.2 us (21%)
  local copies, waits for them, and re-layouts  2.19 us (1%)
    ppermute x32, waiting for transfers between devices, shifted(): return lax.ppermute(x, axis, [(i, (i + step) % n) for i in range(n)])  47.6 us
    ppermute x32, starting transfers between devices, shifted(): return lax.ppermute(x, axis, [(i, (i + step) % n) for i in range(n)])  36.1 us
    pallas_call x2, Pallas kernels, on_device(): pl.pallas_call(attend_kernel, out_shape=(half_shape, half_shape), in_spec...  30 us
    all_to_all x2, starting transfers between devices, exchanged(): return lax.all_to_all(copies, axes, split_axis=0, concat_axis=0, tiled=True)  23.2 us
    ppermute x12, starting transfers between devices, crossed(): lax.ppermute(x, axis, [(i, i ^ bit) for i in range(lax.axis_size(axis))])  19.1 us
    ppermute x12, waiting for transfers between devices, crossed(): lax.ppermute(x, axis, [(i, i ^ bit) for i in range(lax.axis_size(axis))])  6.54 us
  transfers between devices with their start and end apart: 46, of which 21 were waited for; matrix products, arithmetic and copies ran while one was open for 2% of the time, Pallas kernels for 0%

profile of v2, /device:TPU:1, one launch (start us, length us, event | category | flops | bytes accessed | tf_op | source)
XLA Modules:
  0.0 174.9 jit_solution(7104049619251387509)
XLA Ops:
  1.3 1.8 %prepare.1 = (bf16[288,128]{1,0:T(8,128)(2,1)S(1)}, bf16[8,144,128]{2,1,0:T(8,128)(2,1)}, bf16[144,128]{1,0:T(8,128)(2,1)S(1)}) custom-call(s32[1]{0:T(128)} %bitcast.4.at_ref, s32[1,16]{1,0:T(1,128)} %pairs_ref.5, s32[1]{0:T(128)S(6)} %copy.32.counts_ref, s32[32]{0:T(128)} %owner_ref.5, f32[1,128,128]{2,1,0:T(8,128)} %tp_ref.1, f32[1,128]{1,0:T(1,128)} %tl_ref.1, ...), custom_call_target="tpu_custom_call" | custom-call | tf_op jit(solution)/shard_map/prepare/pallas_call | solution.py:334
  3.1 3.3 %collective-permute-start.5 = (bf16[144,128]{1,0:T(8,128)(2,1)S(1)}, bf16[144,128]{1,0:T(8,128)(2,1)S(1)}, u32[]{:S(2)}, u32[]{:S(2)}) collective-permute-start(bf16[144,128]{1,0:T(8,128)(2,1)S(1)} %get-tuple-element.30), channel_id=1, source_target_pairs={{0,192},{64,0},{128,64},{192,128},{1,193},{65,1},{129,65},{193,129... | collective-permute-start | bytes 110600 | tf_op jit(solution)/shard_map/ppermute | solution.py:278
  7.5 8.2 %all-to-all-start = ((bf16[8,144,128]{2,1,0:T(8,128)(2,1)}), bf16[8,144,128]{2,1,0:T(8,128)(2,1)S(1)}, u32[]{:S(2)}, u32[]{:S(2)}) async-start(bf16[8,144,128]{2,1,0:T(8,128)(2,1)} %get-tuple-element.29), calls=%async_computation | async-start | bytes 589824 | tf_op jit(solution)/shard_map/all_to_all | solution.py:273
  15.8 1.5 collective-permute-start.6
  17.3 2.4 %collective-permute-start.13 = (bf16[288,128]{1,0:T(8,128)(2,1)S(1)}, bf16[288,128]{1,0:T(8,128)(2,1)S(1)}, u32[]{:S(2)}, u32[]{:S(2)}) collective-permute-start(bf16[288,128]{1,0:T(8,128)(2,1)S(1)} %get-tuple-element.31), channel_id=1, source_target_pairs={{0,1},{1,0},{2,3},{3,2},{4,5},{5,4},{6,7},{7,6},{8,9},{9,8},{10,11... | collective-permute-start | bytes 221192 | tf_op jit(solution)/shard_map/ppermute | solution.py:282
  19.7 1.0 collective-permute-start.10
  20.7 6.9 %collective-permute-done.6.refs_5_ = bf16[4,144,128]{2,1,0:T(8,128)(2,1)S(1)} collective-permute-done((bf16[4,144,128]{2,1,0:T(8,128)(2,1)S(1)}, bf16[4,144,128]{2,1,0:T(8,128)(2,1)S(1)}, u32[]{:S(2)}, u32[]{:S(2)}) %collective-permute-start.6) | collective-permute-done | bytes 147488 | tf_op jit(solution)/shard_map/ppermute | solution.py:278
  28.2 1.3 collective-permute-start.14
  29.5 2.1 %collective-permute-start.11 = (bf16[4,144,128]{2,1,0:T(8,128)(2,1)S(1)}, bf16[4,144,128]{2,1,0:T(8,128)(2,1)S(1)}, u32[]{:S(2)}, u32[]{:S(2)}) collective-permute-start(bf16[4,144,128]{2,1,0:T(8,128)(2,1)S(1)} %collective-permute-done.10.refs_11_), channel_id=1, source_target_pairs={{0,56},{8,0},{16,8},{24,16},{32,24},{40,32},{48,40},{56,48},{1,57}... | collective-permute-start | bytes 442376 | tf_op jit(solution)/shard_map/ppermute | solution.py:278
  31.7 2.1 %collective-permute-start.2 = (bf16[8,144,128]{2,1,0:T(8,128)(2,1)S(1)}, bf16[8,144,128]{2,1,0:T(8,128)(2,1)S(1)}, u32[]{:S(2)}, u32[]{:S(2)}) collective-permute-start(bf16[8,144,128]{2,1,0:T(8,128)(2,1)S(1)} %all-to-all-done.refs_0_), channel_id=1, source_target_pairs={{0,192},{64,0},{128,64},{192,128},{1,193},{65,1},{129,65},{193,129... | collective-permute-start | bytes 884744 | tf_op jit(solution)/shard_map/ppermute | solution.py:278
  33.8 1.3 collective-permute-start.1
  35.5 3.0 %collective-permute-start.15 = (bf16[4,288,128]{2,1,0:T(8,128)(2,1)S(1)}, bf16[4,288,128]{2,1,0:T(8,128)(2,1)S(1)}, u32[]{:S(2)}, u32[]{:S(2)}) collective-permute-start(bf16[4,288,128]{2,1,0:T(8,128)(2,1)S(1)} %pad_maximum_fusion.refs_12_), channel_id=1, source_target_pairs={{0,4},{2,6},{4,0},{6,2},{1,5},{3,7},{5,1},{7,3},{8,12},{10,14},{12... | collective-permute-start | bytes 884744 | tf_op jit(solution)/shard_map/ppermute | solution.py:282
  39.0 2.2 %collective-permute-start.12 = (bf16[4,144,128]{2,1,0:T(8,128)(2,1)S(1)}, bf16[4,144,128]{2,1,0:T(8,128)(2,1)S(1)}, u32[]{:S(2)}, u32[]{:S(2)}) collective-permute-start(bf16[4,144,128]{2,1,0:T(8,128)(2,1)S(1)} %collective-permute-done.11.refs_10_), channel_id=1, source_target_pairs={{0,56},{8,0},{16,8},{24,16},{32,24},{40,32},{48,40},{56,48},{1,57}... | collective-permute-start | bytes 442376 | tf_op jit(solution)/shard_map/ppermute | solution.py:278
  41.9 8.0 %collective-permute-done.refs_1_ = bf16[8,144,128]{2,1,0:T(8,128)(2,1)S(1)} collective-permute-done((bf16[8,144,128]{2,1,0:T(8,128)(2,1)S(1)}, bf16[8,144,128]{2,1,0:T(8,128)(2,1)S(1)}, u32[]{:S(2)}, u32[]{:S(2)}) %collective-permute-start) | collective-permute-done | bytes 294944 | tf_op jit(solution)/shard_map/ppermute | solution.py:278
  50.7 23.5 %attend.2 = (bf16[4,288,128]{2,1,0:T(8,128)(2,1)S(1)}, bf16[4,288,128]{2,1,0:T(8,128)(2,1)S(1)}) custom-call(s32[4]{0:T(128)} %pad_add_fusion.at_ref, s32[1,16]{1,0:T(1,128)} %pairs_ref.5, s32[1]{0:T(128)S(6)} %copy.32.counts_ref, s32[32]{0:T(128)} %owner_ref.5, s32[32]{0:T(128)} %convert_reduce_fusion.named_ref, bf16[8,144,128]{2,1,0:T(8,128)(2,1)} %copy-done, ...), custom_call_target="tpu_custom_call" | custom-call | tf_op jit(solution)/shard_map/attend/pallas_call | solution.py:357
  74.2 3.1 %collective-permute-start.16 = (bf16[4,288,128]{2,1,0:T(8,128)(2,1)S(1)}, bf16[4,288,128]{2,1,0:T(8,128)(2,1)S(1)}, u32[]{:S(2)}, u32[]{:S(2)}) collective-permute-start(bf16[4,288,128]{2,1,0:T(8,128)(2,1)S(1)} %get-tuple-element.33), channel_id=1, source_target_pairs={{0,1},{1,0},{2,3},{3,2},{4,5},{5,4},{6,7},{7,6},{8,9},{9,8},{10,11... | collective-permute-start | bytes 884744 | tf_op jit(solution)/shard_map/ppermute | solution.py:278
  77.3 1.2 collective-permute-done.16.other_ref
  79.2 2.9 %collective-permute-start.18 = (bf16[288,128]{1,0:T(8,128)(2,1)S(1)}, bf16[288,128]{1,0:T(8,128)(2,1)S(1)}, u32[]{:S(2)}, u32[]{:S(2)}) collective-permute-start(bf16[288,128]{1,0:T(8,128)(2,1)S(1)} %get-tuple-element.36), channel_id=1, source_target_pairs={{0,4},{2,6},{4,0},{6,2},{1,5},{3,7},{5,1},{7,3},{8,12},{10,14},{12... | collective-permute-start | bytes 221192 | tf_op jit(solution)/shard_map/ppermute | solution.py:282
  82.8 1.5 dynamic-slice_bitcast_fusion.refs_5_
  85.3 1.6 collective-permute-done.19.refs_3_
  87.0 2.1 %settle.2 = (f32[128,128]{1,0:T(8,128)S(1)}, f32[1,128]{1,0:T(1,128)}, f32[136,128]{1,0:T(8,128)S(1)}, bf16[288,128]{1,0:T(8,128)(2,1)S(1)}, bf16[8,144,128]{2,1,0:T(8,128)(2,1)}, /*index=5*/bf16[144,128]{1,0:T(8,128)(2,1)S(1)}) custom-call(bf16[288,128]{1,0:T(8,128)(2,1)S(1)} %get-tuple-element.34.refs_0_, ...), custom_call_target="tpu_custom_call" | custom-call | tf_op jit(solution)/shard_map/settle/pallas_call | solution.py:391
  89.1 1.5 collective-permute-start.23
  90.5 1.3 collective-permute-done.25
  91.9 1.5 collective-permute-done.24
  94.3 1.1 collective-permute-start.30
  95.4 15.0 %all-to-all-start.1 = ((bf16[8,144,128]{2,1,0:T(8,128)(2,1)}), bf16[8,144,128]{2,1,0:T(8,128)(2,1)S(1)}, u32[]{:S(2)}, u32[]{:S(2)}) async-start(bf16[8,144,128]{2,1,0:T(8,128)(2,1)} %get-tuple-element.38), calls=%async_computation.1 | async-start | bytes 589824 | tf_op jit(solution)/shard_map/all_to_all | solution.py:273
  110.4 3.6 %collective-permute-start.33 = (bf16[288,128]{1,0:T(8,128)(2,1)S(1)}, bf16[288,128]{1,0:T(8,128)(2,1)S(1)}, u32[]{:S(2)}, u32[]{:S(2)}) collective-permute-start(bf16[288,128]{1,0:T(8,128)(2,1)S(1)} %get-tuple-element.40), channel_id=1, source_target_pairs={{0,1},{1,0},{2,3},{3,2},{4,5},{5,4},{6,7},{7,6},{8,9},{9,8},{10,11... | collective-permute-start | bytes 221192 | tf_op jit(solution)/shard_map/ppermute | solution.py:282
  114.0 1.7 collective-permute-start.26
  115.7 1.3 collective-permute-start.31
  117.2 5.3 %collective-permute-done.26.refs_5_ = bf16[4,144,128]{2,1,0:T(8,128)(2,1)S(1)} collective-permute-done((bf16[4,144,128]{2,1,0:T(8,128)(2,1)S(1)}, bf16[4,144,128]{2,1,0:T(8,128)(2,1)S(1)}, u32[]{:S(2)}, u32[]{:S(2)}) %collective-permute-start.26) | collective-permute-done | bytes 147488 | tf_op jit(solution)/shard_map/ppermute | solution.py:278
  123.2 2.0 %collective-permute-start.32 = (bf16[4,144,128]{2,1,0:T(8,128)(2,1)S(1)}, bf16[4,144,128]{2,1,0:T(8,128)(2,1)S(1)}, u32[]{:S(2)}, u32[]{:S(2)}) collective-permute-start(bf16[4,144,128]{2,1,0:T(8,128)(2,1)S(1)} %collective-permute-done.31.refs_10_), channel_id=1, source_target_pairs={{0,56},{8,0},{16,8},{24,16},{32,24},{40,32},{48,40},{56,48},{1,57}... | collective-permute-start | bytes 442376 | tf_op jit(solution)/shard_map/ppermute | solution.py:278
  126.1 1.6 collective-permute-done.27.refs_6_
  128.4 1.2 collective-permute-start.21
  130.4 2.8 %collective-permute-done.28.refs_7_ = bf16[4,144,128]{2,1,0:T(8,128)(2,1)S(1)} collective-permute-done((bf16[4,144,128]{2,1,0:T(8,128)(2,1)S(1)}, bf16[4,144,128]{2,1,0:T(8,128)(2,1)S(1)}, u32[]{:S(2)}, u32[]{:S(2)}) %collective-permute-start.28) | collective-permute-done | bytes 147488 | tf_op jit(solution)/shard_map/ppermute | solution.py:278
  133.2 5.6 %collective-permute-done.29.refs_8_ = bf16[4,144,128]{2,1,0:T(8,128)(2,1)S(1)} collective-permute-done((bf16[4,144,128]{2,1,0:T(8,128)(2,1)S(1)}, bf16[4,144,128]{2,1,0:T(8,128)(2,1)S(1)}, u32[]{:S(2)}, u32[]{:S(2)}) %collective-permute-start.29) | collective-permute-done | bytes 147488 | tf_op jit(solution)/shard_map/ppermute | solution.py:278
  138.8 4.9 %collective-permute-done.20.refs_1_ = bf16[8,144,128]{2,1,0:T(8,128)(2,1)S(1)} collective-permute-done((bf16[8,144,128]{2,1,0:T(8,128)(2,1)S(1)}, bf16[8,144,128]{2,1,0:T(8,128)(2,1)S(1)}, u32[]{:S(2)}, u32[]{:S(2)}) %collective-permute-start.20) | collective-permute-done | bytes 294944 | tf_op jit(solution)/shard_map/ppermute | solution.py:278
  143.7 6.5 %attend.3 = (bf16[4,288,128]{2,1,0:T(8,128)(2,1)S(1)}, bf16[4,288,128]{2,1,0:T(8,128)(2,1)S(1)}) custom-call(s32[4]{0:T(128)} %pad_add_fusion.at_ref, s32[1,16]{1,0:T(1,128)} %pairs_ref.5, s32[1]{0:T(128)S(6)} %copy.32.counts_ref, s32[32]{0:T(128)} %owner_ref.5, s32[32]{0:T(128)} %convert_reduce_fusion.named_ref, bf16[8,144,128]{2,1,0:T(8,128)(2,1)} %copy-done.1, ...), custom_call_target="tpu_custom_call" | custom-call | tf_op jit(solution)/shard_map/attend/pallas_call | solution.py:357
  150.2 2.1 %collective-permute-start.36 = (bf16[4,288,128]{2,1,0:T(8,128)(2,1)S(1)}, bf16[4,288,128]{2,1,0:T(8,128)(2,1)S(1)}, u32[]{:S(2)}, u32[]{:S(2)}) collective-permute-start(bf16[4,288,128]{2,1,0:T(8,128)(2,1)S(1)} %get-tuple-element.42), channel_id=1, source_target_pairs={{0,1},{1,0},{2,3},{3,2},{4,5},{5,4},{6,7},{7,6},{8,9},{9,8},{10,11... | collective-permute-start | bytes 884744 | tf_op jit(solution)/shard_map/ppermute | solution.py:278
  152.2 1.2 collective-permute-done.36.other_ref
  154.4 2.3 %collective-permute-start.38 = (bf16[288,128]{1,0:T(8,128)(2,1)S(1)}, bf16[288,128]{1,0:T(8,128)(2,1)S(1)}, u32[]{:S(2)}, u32[]{:S(2)}) collective-permute-start(bf16[288,128]{1,0:T(8,128)(2,1)S(1)} %get-tuple-element.45), channel_id=1, source_target_pairs={{0,4},{2,6},{4,0},{6,2},{1,5},{3,7},{5,1},{7,3},{8,12},{10,14},{12... | collective-permute-start | bytes 221192 | tf_op jit(solution)/shard_map/ppermute | solution.py:282
  157.8 2.2 %collective-permute-done.38.refs_2_ = bf16[288,128]{1,0:T(8,128)(2,1)S(1)} collective-permute-done((bf16[288,128]{1,0:T(8,128)(2,1)S(1)}, bf16[288,128]{1,0:T(8,128)(2,1)S(1)}, u32[]{:S(2)}, u32[]{:S(2)}) %collective-permute-start.38) | collective-permute-done | bytes 73760 | tf_op jit(solution)/shard_map/ppermute | solution.py:282
  160.0 1.6 collective-permute-done.39.refs_3_
  162.6 1.1 collective-permute-start.42
  164.3 1.5 collective-permute-done.42
  165.8 2.7 %collective-permute-done.41 = f32[136,128]{1,0:T(8,128)S(1)} collective-permute-done((f32[136,128]{1,0:T(8,128)S(1)}, f32[136,128]{1,0:T(8,128)S(1)}, u32[]{:S(2)}, u32[]{:S(2)}) %collective-permute-start.41) | collective-permute-done | bytes 69664 | tf_op jit(solution)/shard_map/ppermute | solution.py:278
  169.0 3.2 %collective-permute-start.43 = (f32[4,136,128]{2,1,0:T(8,128)S(1)}, f32[4,136,128]{2,1,0:T(8,128)S(1)}, u32[]{:S(2)}, u32[]{:S(2)}) collective-permute-start(f32[4,136,128]{2,1,0:T(8,128)S(1)} %pad_maximum_fusion.2.refs_0_), channel_id=1, source_target_pairs={{0,1},{1,0},{2,3},{3,2},{4,5},{5,4},{6,7},{7,6},{8,9},{9,8},{10,11... | collective-permute-start | bytes 835592 | tf_op jit(solution)/shard_map/ppermute | solution.py:278
  172.2 1.2 collective-permute-done.43.refs_1_
  173.4 1.5 finish.1
  (102 shorter events, 14.5 us)
Async XLA Ops:
  3.1 12.6 %collective-permute-start.5 = (bf16[144,128]{1,0:T(8,128)(2,1)S(1)}, bf16[144,128]{1,0:T(8,128)(2,1)S(1)}, u32[]{:S(2)}, u32[]{:S(2)}) collective-permute-start(bf16[144,128]{1,0:T(8,128)(2,1)S(1)} %get-tuple-element.30), channel_id=1, source_target_pairs={{0,192},{64,0},{128,64},{192,128},{1,193},{65,1},{129,65},{193,129... | collective-permute-start | bytes 110600 | tf_op jit(solution)/shard_map/ppermute | solution.py:278
  6.4 9.3 %collective-permute-start.4 = (bf16[144,128]{1,0:T(8,128)(2,1)S(1)}, bf16[144,128]{1,0:T(8,128)(2,1)S(1)}, u32[]{:S(2)}, u32[]{:S(2)}) collective-permute-start(bf16[144,128]{1,0:T(8,128)(2,1)S(1)} %get-tuple-element.30), channel_id=1, source_target_pairs={{0,128},{64,192},{128,0},{192,64},{1,129},{65,193},{129,1},{193,65... | collective-permute-start | bytes 110600 | tf_op jit(solution)/shard_map/ppermute | solution.py:278
  6.9 8.8 %collective-permute-start.3 = (bf16[144,128]{1,0:T(8,128)(2,1)S(1)}, bf16[144,128]{1,0:T(8,128)(2,1)S(1)}, u32[]{:S(2)}, u32[]{:S(2)}) collective-permute-start(bf16[144,128]{1,0:T(8,128)(2,1)S(1)} %get-tuple-element.30), channel_id=1, source_target_pairs={{0,64},{64,128},{128,192},{192,0},{1,65},{65,129},{129,193},{193,1... | collective-permute-start | bytes 110600 | tf_op jit(solution)/shard_map/ppermute | solution.py:278
  7.5 24.1 %all-to-all-start = ((bf16[8,144,128]{2,1,0:T(8,128)(2,1)}), bf16[8,144,128]{2,1,0:T(8,128)(2,1)S(1)}, u32[]{:S(2)}, u32[]{:S(2)}) async-start(bf16[8,144,128]{2,1,0:T(8,128)(2,1)} %get-tuple-element.29), calls=%async_computation | async-start | bytes 589824 | tf_op jit(solution)/shard_map/all_to_all | solution.py:273
  15.8 11.8 %collective-permute-start.6 = (bf16[4,144,128]{2,1,0:T(8,128)(2,1)S(1)}, bf16[4,144,128]{2,1,0:T(8,128)(2,1)S(1)}, u32[]{:S(2)}, u32[]{:S(2)}) collective-permute-start(bf16[4,144,128]{2,1,0:T(8,128)(2,1)S(1)} %pad_maximum_fusion.3.refs_4_), channel_id=1, source_target_pairs={{0,8},{8,16},{16,24},{24,32},{32,40},{40,48},{48,56},{56,0},{1,9},... | collective-permute-start | bytes 442376 | tf_op jit(solution)/shard_map/ppermute | solution.py:278
  17.3 10.3 %collective-permute-start.13 = (bf16[288,128]{1,0:T(8,128)(2,1)S(1)}, bf16[288,128]{1,0:T(8,128)(2,1)S(1)}, u32[]{:S(2)}, u32[]{:S(2)}) collective-permute-start(bf16[288,128]{1,0:T(8,128)(2,1)S(1)} %get-tuple-element.31), channel_id=1, source_target_pairs={{0,1},{1,0},{2,3},{3,2},{4,5},{5,4},{6,7},{7,6},{8,9},{9,8},{10,11... | collective-permute-start | bytes 221192 | tf_op jit(solution)/shard_map/ppermute | solution.py:282
  19.7 9.9 %collective-permute-start.10 = (bf16[4,144,128]{2,1,0:T(8,128)(2,1)S(1)}, bf16[4,144,128]{2,1,0:T(8,128)(2,1)S(1)}, u32[]{:S(2)}, u32[]{:S(2)}) collective-permute-start(bf16[4,144,128]{2,1,0:T(8,128)(2,1)S(1)} %pad_maximum_fusion.3.refs_4_), channel_id=1, source_target_pairs={{0,56},{8,0},{16,8},{24,16},{32,24},{40,32},{48,40},{56,48},{1,57}... | collective-permute-start | bytes 442376 | tf_op jit(solution)/shard_map/ppermute | solution.py:278
  27.6 6.2 %collective-permute-start.7 = (bf16[4,144,128]{2,1,0:T(8,128)(2,1)S(1)}, bf16[4,144,128]{2,1,0:T(8,128)(2,1)S(1)}, u32[]{:S(2)}, u32[]{:S(2)}) collective-permute-start(bf16[4,144,128]{2,1,0:T(8,128)(2,1)S(1)} %collective-permute-done.6.refs_5_), channel_id=1, source_target_pairs={{0,8},{8,16},{16,24},{24,32},{32,40},{40,48},{48,56},{56,0},{1,9},... | collective-permute-start | bytes 442376 | tf_op jit(solution)/shard_map/ppermute | solution.py:278
  28.2 6.9 %collective-permute-start.14 = (bf16[2,288,128]{2,1,0:T(8,128)(2,1)S(1)}, bf16[2,288,128]{2,1,0:T(8,128)(2,1)S(1)}, u32[]{:S(2)}, u32[]{:S(2)}) collective-permute-start(bf16[2,288,128]{2,1,0:T(8,128)(2,1)S(1)} %pad_maximum_fusion.4), channel_id=1, source_target_pairs={{0,2},{2,0},{4,6},{6,4},{1,3},{3,1},{5,7},{7,5},{8,10},{10,8},{12,... | collective-permute-start | bytes 442376 | tf_op jit(solution)/shard_map/ppermute | solution.py:282
  29.5 6.0 %collective-permute-start.11 = (bf16[4,144,128]{2,1,0:T(8,128)(2,1)S(1)}, bf16[4,144,128]{2,1,0:T(8,128)(2,1)S(1)}, u32[]{:S(2)}, u32[]{:S(2)}) collective-permute-start(bf16[4,144,128]{2,1,0:T(8,128)(2,1)S(1)} %collective-permute-done.10.refs_11_), channel_id=1, source_target_pairs={{0,56},{8,0},{16,8},{24,16},{32,24},{40,32},{48,40},{56,48},{1,57}... | collective-permute-start | bytes 442376 | tf_op jit(solution)/shard_map/ppermute | solution.py:278
  31.7 9.5 %collective-permute-start.2 = (bf16[8,144,128]{2,1,0:T(8,128)(2,1)S(1)}, bf16[8,144,128]{2,1,0:T(8,128)(2,1)S(1)}, u32[]{:S(2)}, u32[]{:S(2)}) collective-permute-start(bf16[8,144,128]{2,1,0:T(8,128)(2,1)S(1)} %all-to-all-done.refs_0_), channel_id=1, source_target_pairs={{0,192},{64,0},{128,64},{192,128},{1,193},{65,1},{129,65},{193,129... | collective-permute-start | bytes 884744 | tf_op jit(solution)/shard_map/ppermute | solution.py:278
  33.8 5.2 %collective-permute-start.8 = (bf16[4,144,128]{2,1,0:T(8,128)(2,1)S(1)}, bf16[4,144,128]{2,1,0:T(8,128)(2,1)S(1)}, u32[]{:S(2)}, u32[]{:S(2)}) collective-permute-start(bf16[4,144,128]{2,1,0:T(8,128)(2,1)S(1)} %collective-permute-done.7.refs_6_), channel_id=1, source_target_pairs={{0,8},{8,16},{16,24},{24,32},{32,40},{40,48},{48,56},{56,0},{1,9},... | collective-permute-start | bytes 442376 | tf_op jit(solution)/shard_map/ppermute | solution.py:278
  33.8 8.1 %collective-permute-start.1 = (bf16[8,144,128]{2,1,0:T(8,128)(2,1)S(1)}, bf16[8,144,128]{2,1,0:T(8,128)(2,1)S(1)}, u32[]{:S(2)}, u32[]{:S(2)}) collective-permute-start(bf16[8,144,128]{2,1,0:T(8,128)(2,1)S(1)} %all-to-all-done.refs_0_), channel_id=1, source_target_pairs={{0,128},{64,192},{128,0},{192,64},{1,129},{65,193},{129,1},{193,65... | collective-permute-start | bytes 884744 | tf_op jit(solution)/shard_map/ppermute | solution.py:278
  35.1 14.8 %collective-permute-start = (bf16[8,144,128]{2,1,0:T(8,128)(2,1)S(1)}, bf16[8,144,128]{2,1,0:T(8,128)(2,1)S(1)}, u32[]{:S(2)}, u32[]{:S(2)}) collective-permute-start(bf16[8,144,128]{2,1,0:T(8,128)(2,1)S(1)} %all-to-all-done.refs_0_), channel_id=1, source_target_pairs={{0,64},{64,128},{128,192},{192,0},{1,65},{65,129},{129,193},{193,1... | collective-permute-start | bytes 884744 | tf_op jit(solution)/shard_map/ppermute | solution.py:278
  35.5 15.1 %collective-permute-start.15 = (bf16[4,288,128]{2,1,0:T(8,128)(2,1)S(1)}, bf16[4,288,128]{2,1,0:T(8,128)(2,1)S(1)}, u32[]{:S(2)}, u32[]{:S(2)}) collective-permute-start(bf16[4,288,128]{2,1,0:T(8,128)(2,1)S(1)} %pad_maximum_fusion.refs_12_), channel_id=1, source_target_pairs={{0,4},{2,6},{4,0},{6,2},{1,5},{3,7},{5,1},{7,3},{8,12},{10,14},{12... | collective-permute-start | bytes 884744 | tf_op jit(solution)/shard_map/ppermute | solution.py:282
  39.0 11.7 %collective-permute-start.12 = (bf16[4,144,128]{2,1,0:T(8,128)(2,1)S(1)}, bf16[4,144,128]{2,1,0:T(8,128)(2,1)S(1)}, u32[]{:S(2)}, u32[]{:S(2)}) collective-permute-start(bf16[4,144,128]{2,1,0:T(8,128)(2,1)S(1)} %collective-permute-done.11.refs_10_), channel_id=1, source_target_pairs={{0,56},{8,0},{16,8},{24,16},{32,24},{40,32},{48,40},{56,48},{1,57}... | collective-permute-start | bytes 442376 | tf_op jit(solution)/shard_map/ppermute | solution.py:278
  41.2 9.4 %collective-permute-start.9 = (bf16[4,144,128]{2,1,0:T(8,128)(2,1)S(1)}, bf16[4,144,128]{2,1,0:T(8,128)(2,1)S(1)}, u32[]{:S(2)}, u32[]{:S(2)}) collective-permute-start(bf16[4,144,128]{2,1,0:T(8,128)(2,1)S(1)} %collective-permute-done.8.refs_7_), channel_id=1, source_target_pairs={{0,8},{8,16},{16,24},{24,32},{32,40},{40,48},{48,56},{56,0},{1,9},... | collective-permute-start | bytes 442376 | tf_op jit(solution)/shard_map/ppermute | solution.py:278
  74.2 4.3 %collective-permute-start.16 = (bf16[4,288,128]{2,1,0:T(8,128)(2,1)S(1)}, bf16[4,288,128]{2,1,0:T(8,128)(2,1)S(1)}, u32[]{:S(2)}, u32[]{:S(2)}) collective-permute-start(bf16[4,288,128]{2,1,0:T(8,128)(2,1)S(1)} %get-tuple-element.33), channel_id=1, source_target_pairs={{0,1},{1,0},{2,3},{3,2},{4,5},{5,4},{6,7},{7,6},{8,9},{9,8},{10,11... | collective-permute-start | bytes 884744 | tf_op jit(solution)/shard_map/ppermute | solution.py:278
  78.9 5.4 %collective-permute-start.17 = (bf16[288,128]{1,0:T(8,128)(2,1)S(1)}, bf16[288,128]{1,0:T(8,128)(2,1)S(1)}, u32[]{:S(2)}, u32[]{:S(2)}) collective-permute-start(bf16[288,128]{1,0:T(8,128)(2,1)S(1)} %get-tuple-element.35), channel_id=1, source_target_pairs={{0,2},{2,0},{4,6},{6,4},{1,3},{3,1},{5,7},{7,5},{8,10},{10,8},{12,... | collective-permute-start | bytes 221192 | tf_op jit(solution)/shard_map/ppermute | solution.py:282
  79.2 6.2 %collective-permute-start.18 = (bf16[288,128]{1,0:T(8,128)(2,1)S(1)}, bf16[288,128]{1,0:T(8,128)(2,1)S(1)}, u32[]{:S(2)}, u32[]{:S(2)}) collective-permute-start(bf16[288,128]{1,0:T(8,128)(2,1)S(1)} %get-tuple-element.36), channel_id=1, source_target_pairs={{0,4},{2,6},{4,0},{6,2},{1,5},{3,7},{5,1},{7,3},{8,12},{10,14},{12... | collective-permute-start | bytes 221192 | tf_op jit(solution)/shard_map/ppermute | solution.py:282
  82.1 4.9 %collective-permute-start.19 = (bf16[288,128]{1,0:T(8,128)(2,1)S(1)}, bf16[288,128]{1,0:T(8,128)(2,1)S(1)}, u32[]{:S(2)}, u32[]{:S(2)}) collective-permute-start(bf16[288,128]{1,0:T(8,128)(2,1)S(1)} %get-tuple-element.37), channel_id=1, source_target_pairs={{0,6},{2,4},{4,2},{6,0},{1,7},{3,5},{5,3},{7,1},{8,14},{10,12},{12... | collective-permute-start | bytes 221192 | tf_op jit(solution)/shard_map/ppermute | solution.py:282
  89.1 2.8 %collective-permute-start.25 = (bf16[144,128]{1,0:T(8,128)(2,1)S(1)}, bf16[144,128]{1,0:T(8,128)(2,1)S(1)}, u32[]{:S(2)}, u32[]{:S(2)}) collective-permute-start(bf16[144,128]{1,0:T(8,128)(2,1)S(1)} %get-tuple-element.39), channel_id=1, source_target_pairs={{0,192},{64,0},{128,64},{192,128},{1,193},{65,1},{129,65},{193,129... | collective-permute-start | bytes 110600 | tf_op jit(solution)/shard_map/ppermute | solution.py:278
  89.1 4.3 %collective-permute-start.24 = (bf16[144,128]{1,0:T(8,128)(2,1)S(1)}, bf16[144,128]{1,0:T(8,128)(2,1)S(1)}, u32[]{:S(2)}, u32[]{:S(2)}) collective-permute-start(bf16[144,128]{1,0:T(8,128)(2,1)S(1)} %get-tuple-element.39), channel_id=1, source_target_pairs={{0,128},{64,192},{128,0},{192,64},{1,129},{65,193},{129,1},{193,65... | collective-permute-start | bytes 110600 | tf_op jit(solution)/shard_map/ppermute | solution.py:278
  89.1 5.2 %collective-permute-start.23 = (bf16[144,128]{1,0:T(8,128)(2,1)S(1)}, bf16[144,128]{1,0:T(8,128)(2,1)S(1)}, u32[]{:S(2)}, u32[]{:S(2)}) collective-permute-start(bf16[144,128]{1,0:T(8,128)(2,1)S(1)} %get-tuple-element.39), channel_id=1, source_target_pairs={{0,64},{64,128},{128,192},{192,0},{1,65},{65,129},{129,193},{193,1... | collective-permute-start | bytes 110600 | tf_op jit(solution)/shard_map/ppermute | solution.py:278
  94.3 19.7 %copy-start.5 = (bf16[4,144,128]{2,1,0:T(8,128)(2,1)}, bf16[4,144,128]{2,1,0:T(8,128)(2,1)S(1)}, u32[]{:S(2)}) copy-start(bf16[4,144,128]{2,1,0:T(8,128)(2,1)S(1)} %pad_maximum_fusion.5.refs_4_) | copy-start | bytes 442372
  94.3 21.4 %collective-permute-start.30 = (bf16[4,144,128]{2,1,0:T(8,128)(2,1)S(1)}, bf16[4,144,128]{2,1,0:T(8,128)(2,1)S(1)}, u32[]{:S(2)}, u32[]{:S(2)}) collective-permute-start(bf16[4,144,128]{2,1,0:T(8,128)(2,1)S(1)} %pad_maximum_fusion.5.refs_4_), channel_id=1, source_target_pairs={{0,56},{8,0},{16,8},{24,16},{32,24},{40,32},{48,40},{56,48},{1,57}... | collective-permute-start | bytes 442376 | tf_op jit(solution)/shard_map/ppermute | solution.py:278
  95.4 32.3 %all-to-all-start.1 = ((bf16[8,144,128]{2,1,0:T(8,128)(2,1)}), bf16[8,144,128]{2,1,0:T(8,128)(2,1)S(1)}, u32[]{:S(2)}, u32[]{:S(2)}) async-start(bf16[8,144,128]{2,1,0:T(8,128)(2,1)} %get-tuple-element.38), calls=%async_computation.1 | async-start | bytes 589824 | tf_op jit(solution)/shard_map/all_to_all | solution.py:273
  110.4 6.6 %collective-permute-start.33 = (bf16[288,128]{1,0:T(8,128)(2,1)S(1)}, bf16[288,128]{1,0:T(8,128)(2,1)S(1)}, u32[]{:S(2)}, u32[]{:S(2)}) collective-permute-start(bf16[288,128]{1,0:T(8,128)(2,1)S(1)} %get-tuple-element.40), channel_id=1, source_target_pairs={{0,1},{1,0},{2,3},{3,2},{4,5},{5,4},{6,7},{7,6},{8,9},{9,8},{10,11... | collective-permute-start | bytes 221192 | tf_op jit(solution)/shard_map/ppermute | solution.py:282
  114.0 8.5 %collective-permute-start.26 = (bf16[4,144,128]{2,1,0:T(8,128)(2,1)S(1)}, bf16[4,144,128]{2,1,0:T(8,128)(2,1)S(1)}, u32[]{:S(2)}, u32[]{:S(2)}) collective-permute-start(bf16[4,144,128]{2,1,0:T(8,128)(2,1)S(1)} %pad_maximum_fusion.5.refs_4_), channel_id=1, source_target_pairs={{0,8},{8,16},{16,24},{24,32},{32,40},{40,48},{48,56},{56,0},{1,9},... | collective-permute-start | bytes 442376 | tf_op jit(solution)/shard_map/ppermute | solution.py:278
  115.7 7.4 %collective-permute-start.31 = (bf16[4,144,128]{2,1,0:T(8,128)(2,1)S(1)}, bf16[4,144,128]{2,1,0:T(8,128)(2,1)S(1)}, u32[]{:S(2)}, u32[]{:S(2)}) collective-permute-start(bf16[4,144,128]{2,1,0:T(8,128)(2,1)S(1)} %collective-permute-done.30.refs_11_), channel_id=1, source_target_pairs={{0,56},{8,0},{16,8},{24,16},{32,24},{40,32},{48,40},{56,48},{1,57}... | collective-permute-start | bytes 442376 | tf_op jit(solution)/shard_map/ppermute | solution.py:278
  117.1 8.1 %collective-permute-start.34 = (bf16[2,288,128]{2,1,0:T(8,128)(2,1)S(1)}, bf16[2,288,128]{2,1,0:T(8,128)(2,1)S(1)}, u32[]{:S(2)}, u32[]{:S(2)}) collective-permute-start(bf16[2,288,128]{2,1,0:T(8,128)(2,1)S(1)} %pad_maximum_fusion.6), channel_id=1, source_target_pairs={{0,2},{2,0},{4,6},{6,4},{1,3},{3,1},{5,7},{7,5},{8,10},{10,8},{12,... | collective-permute-start | bytes 442376 | tf_op jit(solution)/shard_map/ppermute | solution.py:282
  122.5 5.2 %collective-permute-start.27 = (bf16[4,144,128]{2,1,0:T(8,128)(2,1)S(1)}, bf16[4,144,128]{2,1,0:T(8,128)(2,1)S(1)}, u32[]{:S(2)}, u32[]{:S(2)}) collective-permute-start(bf16[4,144,128]{2,1,0:T(8,128)(2,1)S(1)} %collective-permute-done.26.refs_5_), channel_id=1, source_target_pairs={{0,8},{8,16},{16,24},{24,32},{32,40},{40,48},{48,56},{56,0},{1,9},... | collective-permute-start | bytes 442376 | tf_op jit(solution)/shard_map/ppermute | solution.py:278
  123.2 6.4 %collective-permute-start.32 = (bf16[4,144,128]{2,1,0:T(8,128)(2,1)S(1)}, bf16[4,144,128]{2,1,0:T(8,128)(2,1)S(1)}, u32[]{:S(2)}, u32[]{:S(2)}) collective-permute-start(bf16[4,144,128]{2,1,0:T(8,128)(2,1)S(1)} %collective-permute-done.31.refs_10_), channel_id=1, source_target_pairs={{0,56},{8,0},{16,8},{24,16},{32,24},{40,32},{48,40},{56,48},{1,57}... | collective-permute-start | bytes 442376 | tf_op jit(solution)/shard_map/ppermute | solution.py:278
  125.2 18.4 %copy-start.3 = (bf16[4,288,128]{2,1,0:T(8,128)(2,1)}, bf16[4,288,128]{2,1,0:T(8,128)(2,1)S(1)}, u32[]{:S(2)}) copy-start(bf16[4,288,128]{2,1,0:T(8,128)(2,1)S(1)} %pad_maximum_fusion.1.refs_12_) | copy-start | bytes 884740
  125.3 8.0 %collective-permute-start.35 = (bf16[4,288,128]{2,1,0:T(8,128)(2,1)S(1)}, bf16[4,288,128]{2,1,0:T(8,128)(2,1)S(1)}, u32[]{:S(2)}, u32[]{:S(2)}) collective-permute-start(bf16[4,288,128]{2,1,0:T(8,128)(2,1)S(1)} %pad_maximum_fusion.1.refs_12_), channel_id=1, source_target_pairs={{0,4},{2,6},{4,0},{6,2},{1,5},{3,7},{5,1},{7,3},{8,12},{10,14},{12... | collective-permute-start | bytes 884744 | tf_op jit(solution)/shard_map/ppermute | solution.py:282
  127.7 5.5 %collective-permute-start.28 = (bf16[4,144,128]{2,1,0:T(8,128)(2,1)S(1)}, bf16[4,144,128]{2,1,0:T(8,128)(2,1)S(1)}, u32[]{:S(2)}, u32[]{:S(2)}) collective-permute-start(bf16[4,144,128]{2,1,0:T(8,128)(2,1)S(1)} %collective-permute-done.27.refs_6_), channel_id=1, source_target_pairs={{0,8},{8,16},{16,24},{24,32},{32,40},{40,48},{48,56},{56,0},{1,9},... | collective-permute-start | bytes 442376 | tf_op jit(solution)/shard_map/ppermute | solution.py:278
  127.7 11.1 %collective-permute-start.22 = (bf16[8,144,128]{2,1,0:T(8,128)(2,1)S(1)}, bf16[8,144,128]{2,1,0:T(8,128)(2,1)S(1)}, u32[]{:S(2)}, u32[]{:S(2)}) collective-permute-start(bf16[8,144,128]{2,1,0:T(8,128)(2,1)S(1)} %all-to-all-done.1.refs_0_), channel_id=1, source_target_pairs={{0,192},{64,0},{128,64},{192,128},{1,193},{65,1},{129,65},{193,129... | collective-permute-start | bytes 884744 | tf_op jit(solution)/shard_map/ppermute | solution.py:278
  128.4 10.4 %collective-permute-start.21 = (bf16[8,144,128]{2,1,0:T(8,128)(2,1)S(1)}, bf16[8,144,128]{2,1,0:T(8,128)(2,1)S(1)}, u32[]{:S(2)}, u32[]{:S(2)}) collective-permute-start(bf16[8,144,128]{2,1,0:T(8,128)(2,1)S(1)} %all-to-all-done.1.refs_0_), channel_id=1, source_target_pairs={{0,128},{64,192},{128,0},{192,64},{1,129},{65,193},{129,1},{193,65... | collective-permute-start | bytes 884744 | tf_op jit(solution)/shard_map/ppermute | solution.py:278
  129.6 14.1 %collective-permute-start.20 = (bf16[8,144,128]{2,1,0:T(8,128)(2,1)S(1)}, bf16[8,144,128]{2,1,0:T(8,128)(2,1)S(1)}, u32[]{:S(2)}, u32[]{:S(2)}) collective-permute-start(bf16[8,144,128]{2,1,0:T(8,128)(2,1)S(1)} %all-to-all-done.1.refs_0_), channel_id=1, source_target_pairs={{0,64},{64,128},{128,192},{192,0},{1,65},{65,129},{129,193},{193,1... | collective-permute-start | bytes 884744 | tf_op jit(solution)/shard_map/ppermute | solution.py:278
  133.2 5.6 %collective-permute-start.29 = (bf16[4,144,128]{2,1,0:T(8,128)(2,1)S(1)}, bf16[4,144,128]{2,1,0:T(8,128)(2,1)S(1)}, u32[]{:S(2)}, u32[]{:S(2)}) collective-permute-start(bf16[4,144,128]{2,1,0:T(8,128)(2,1)S(1)} %collective-permute-done.28.refs_7_), channel_id=1, source_target_pairs={{0,8},{8,16},{16,24},{24,32},{32,40},{40,48},{48,56},{56,0},{1,9},... | collective-permute-start | bytes 442376 | tf_op jit(solution)/shard_map/ppermute | solution.py:278
  150.2 3.3 %collective-permute-start.36 = (bf16[4,288,128]{2,1,0:T(8,128)(2,1)S(1)}, bf16[4,288,128]{2,1,0:T(8,128)(2,1)S(1)}, u32[]{:S(2)}, u32[]{:S(2)}) collective-permute-start(bf16[4,288,128]{2,1,0:T(8,128)(2,1)S(1)} %get-tuple-element.42), channel_id=1, source_target_pairs={{0,1},{1,0},{2,3},{3,2},{4,5},{5,4},{6,7},{7,6},{8,9},{9,8},{10,11... | collective-permute-start | bytes 884744 | tf_op jit(solution)/shard_map/ppermute | solution.py:278
  153.8 3.9 %collective-permute-start.37 = (bf16[288,128]{1,0:T(8,128)(2,1)S(1)}, bf16[288,128]{1,0:T(8,128)(2,1)S(1)}, u32[]{:S(2)}, u32[]{:S(2)}) collective-permute-start(bf16[288,128]{1,0:T(8,128)(2,1)S(1)} %get-tuple-element.44), channel_id=1, source_target_pairs={{0,2},{2,0},{4,6},{6,4},{1,3},{3,1},{5,7},{7,5},{8,10},{10,8},{12,... | collective-permute-start | bytes 221192 | tf_op jit(solution)/shard_map/ppermute | solution.py:282
  154.4 5.6 %collective-permute-start.38 = (bf16[288,128]{1,0:T(8,128)(2,1)S(1)}, bf16[288,128]{1,0:T(8,128)(2,1)S(1)}, u32[]{:S(2)}, u32[]{:S(2)}) collective-permute-start(bf16[288,128]{1,0:T(8,128)(2,1)S(1)} %get-tuple-element.45), channel_id=1, source_target_pairs={{0,4},{2,6},{4,0},{6,2},{1,5},{3,7},{5,1},{7,3},{8,12},{10,14},{12... | collective-permute-start | bytes 221192 | tf_op jit(solution)/shard_map/ppermute | solution.py:282
  156.8 4.9 %collective-permute-start.39 = (bf16[288,128]{1,0:T(8,128)(2,1)S(1)}, bf16[288,128]{1,0:T(8,128)(2,1)S(1)}, u32[]{:S(2)}, u32[]{:S(2)}) collective-permute-start(bf16[288,128]{1,0:T(8,128)(2,1)S(1)} %get-tuple-element.46), channel_id=1, source_target_pairs={{0,6},{2,4},{4,2},{6,0},{1,7},{3,5},{5,3},{7,1},{8,14},{10,12},{12... | collective-permute-start | bytes 221192 | tf_op jit(solution)/shard_map/ppermute | solution.py:282
  162.6 3.2 %collective-permute-start.42 = (f32[136,128]{1,0:T(8,128)S(1)}, f32[136,128]{1,0:T(8,128)S(1)}, u32[]{:S(2)}, u32[]{:S(2)}) collective-permute-start(f32[136,128]{1,0:T(8,128)S(1)} %get-tuple-element.49), channel_id=1, source_target_pairs={{0,6},{2,0},{4,2},{6,4},{1,7},{3,1},{5,3},{7,5},{8,14},{10,8},{12,... | collective-permute-start | bytes 208904 | tf_op jit(solution)/shard_map/ppermute | solution.py:278
  163.7 4.8 %collective-permute-start.41 = (f32[136,128]{1,0:T(8,128)S(1)}, f32[136,128]{1,0:T(8,128)S(1)}, u32[]{:S(2)}, u32[]{:S(2)}) collective-permute-start(f32[136,128]{1,0:T(8,128)S(1)} %get-tuple-element.49), channel_id=1, source_target_pairs={{0,4},{2,6},{4,0},{6,2},{1,5},{3,7},{5,1},{7,3},{8,12},{10,14},{12... | collective-permute-start | bytes 208904 | tf_op jit(solution)/shard_map/ppermute | solution.py:278
  163.7 5.2 %collective-permute-start.40 = (f32[136,128]{1,0:T(8,128)S(1)}, f32[136,128]{1,0:T(8,128)S(1)}, u32[]{:S(2)}, u32[]{:S(2)}) collective-permute-start(f32[136,128]{1,0:T(8,128)S(1)} %get-tuple-element.49), channel_id=1, source_target_pairs={{0,2},{2,4},{4,6},{6,0},{1,3},{3,5},{5,7},{7,1},{8,10},{10,12},{12... | collective-permute-start | bytes 208904 | tf_op jit(solution)/shard_map/ppermute | solution.py:278
  169.0 4.4 %collective-permute-start.43 = (f32[4,136,128]{2,1,0:T(8,128)S(1)}, f32[4,136,128]{2,1,0:T(8,128)S(1)}, u32[]{:S(2)}, u32[]{:S(2)}) collective-permute-start(f32[4,136,128]{2,1,0:T(8,128)S(1)} %pad_maximum_fusion.2.refs_0_), channel_id=1, source_target_pairs={{0,1},{1,0},{2,3},{3,2},{4,5},{5,4},{6,7},{7,6},{8,9},{9,8},{10,11... | collective-permute-start | bytes 835592 | tf_op jit(solution)/shard_map/ppermute | solution.py:278
  (14 other events, 120.7 us)
